TPU v7x, 32 devices: a 4x4x1 block of a 4x4x8 slice. The times are simulated.
32 devices in a mesh: dp: 1 (over z), ep: 32 (over y, x, core).
Axes of the slice: x: 4, y: 4, z: 1, core: 2. Of those that a mesh axis runs over, the one named last changes fastest.
The devices are a block of a 4x4x8 slice.
Arguments:
- hidden: bfloat16 [8192, 2048], P(('dp', 'ep'))
- router_w: float32 [2048, 32], replicated
- expert_ids: int32 [8192, 2], P(('dp', 'ep'))
- w_gate: bfloat16 [32, 2048, 2048], P('ep')
- w_up: bfloat16 [32, 2048, 2048], P('ep')
- w_down: bfloat16 [32, 2048, 2048], P('ep')
- post_scale: float32 [2], replicated
Outputs:
- output: bfloat16 [8192, 2048], P(('dp', 'ep'))
All inputs are finite; a program needn't handle non-finite values.
Results may differ from a plain program's by a relative error of at most 0.001.
Values are sent between devices in bfloat16 or wider.
A program may use at most 768 MiB of HBM per device.

v0:
```python
import jax
import jax.numpy as jnp
from jax import lax
from jax.sharding import PartitionSpec as P


def route_tables(hidden, router_w, expert_ids, experts, capacity):
    tokens, choice_count = expert_ids.shape
    logits = jnp.dot(hidden.astype(jnp.float32), router_w, precision=lax.Precision.HIGHEST, preferred_element_type=jnp.float32)
    router_prob = jax.nn.softmax(logits, axis=-1)
    pick_mask = expert_ids[:, :, None] == jnp.arange(experts, dtype=jnp.int32)[None, None, :]
    picked = jnp.sum(jnp.where(pick_mask, router_prob[:, None, :], 0.0), axis=-1)
    gates = picked / jnp.sum(picked, axis=1, keepdims=True)
    pair_hot = pick_mask.reshape(tokens * choice_count, experts).astype(jnp.int32)
    earlier = jnp.cumsum(pair_hot, axis=0) - pair_hot
    slot_of = jnp.sum(earlier * pair_hot, axis=1).reshape(tokens, choice_count)
    slot_mask = slot_of[:, :, None] == jnp.arange(capacity, dtype=jnp.int32)[None, None, :]
    place = pick_mask[:, :, :, None] & slot_mask[:, :, None, :]
    return gates, place


def solution(mesh):
    ep_size = mesh.shape['ep']

    def local_step(hidden, router_w, expert_ids, w_gate, w_up, w_down, post_scale):
        tokens, model_width = hidden.shape
        local_experts = w_gate.shape[0]
        experts = local_experts * ep_size
        capacity = tokens // max(1, experts // 8)
        gates, place = route_tables(hidden, router_w, expert_ids, experts, capacity)
        token_table = jnp.any(place, axis=1).astype(jnp.bfloat16)
        outgoing = jnp.einsum('tec,td->ecd', token_table, hidden, preferred_element_type=jnp.float32).astype(jnp.bfloat16)
        incoming = lax.all_to_all(outgoing, 'ep', 0, 0, tiled=True).reshape(ep_size, local_experts, capacity, model_width)
        gate_in = jnp.einsum('slcd,ldf->slcf', incoming, w_gate, preferred_element_type=jnp.float32)
        up_in = jnp.einsum('slcd,ldf->slcf', incoming, w_up, preferred_element_type=jnp.float32)
        middle = (jax.nn.silu(gate_in) * up_in).astype(jnp.bfloat16)
        expert_out = jnp.einsum('slcf,lfd->slcd', middle, w_down, preferred_element_type=jnp.float32).astype(jnp.bfloat16)
        returned = lax.all_to_all(expert_out.reshape(experts, capacity, model_width), 'ep', 0, 0, tiled=True)
        pair_out = jnp.einsum('tkec,ecd->tkd', place.astype(jnp.bfloat16), returned, preferred_element_type=jnp.float32)
        mixed = jnp.sum(gates[:, :, None] * pair_out, axis=1)
        result = post_scale[0] * hidden.astype(jnp.float32) + post_scale[1] * mixed
        return result.astype(jnp.bfloat16)

    tok_spec = P(('dp', 'ep'))
    return jax.shard_map(local_step, mesh=mesh, in_specs=(tok_spec, P(), tok_spec, P('ep'), P('ep'), P('ep'), P()), out_specs=tok_spec, check_vma=False)
```

profile of v0, /device:TPU:103, one launch (start us, length us, event | category | flops | bytes accessed | tf_op | source)
XLA Modules:
  0.0 314.7 jit_solution(16820463481267704452)
XLA Ops:
  0.0 0.9 copy.8
  0.9 0.1 eq.58
  1.0 0.1 eq.62
  1.2 0.7 iota_compare_fusion.3
  1.9 1.2 reduce-window.6
  3.0 0.2 slice_reduce_fusion
  3.3 0.1 fusion.30
  3.4 0.1 eq.66
  3.6 0.1 copy.11
  3.7 0.6 copy-done.2
  4.3 0.5 and_reduce_fusion
  4.8 3.7 %convolution_convert_fusion = bf16[32,64,2048]{2,1,0:T(8,128)(2,1)S(1)} fusion(pred[256,32,64]{0,2,1:T(8,128)(4,1)S(1)} %and_reduce_fusion, bf16[256,2048]{1,0:T(8,128)(2,1)} %param.7), kind=kOutput, calls=%fused_computation.17 | convolution fusion | flops 2151677952 | bytes 9961472 | tf_op jit(solution)/shard_map/tec,td->ecd/dot_general | solution.py:32
  8.6 0.0 slice-start.1
  8.6 108.5 %all_to_all.10 = bf16[32,64,2048]{2,1,0:T(8,128)(2,1)S(1)} all-to-all(bf16[32,64,2048]{2,1,0:T(8,128)(2,1)S(1)} %convolution_convert_fusion), channel_id=1, replica_groups=mesh['dp'=1,'ep'=32] {'ep'}, dimensions={0} | all-to-all | bytes 16777216 | tf_op jit(solution)/shard_map/all_to_all | solution.py:33
  117.2 0.0 slice-start.3
  117.2 20.0 %fusion.9 = f32[32,64,2048]{2,1,0:T(8,128)} fusion(bf16[32,64,2048]{2,1,0:T(8,128)(2,1)S(1)} %all_to_all.10, bf16[1,2048,2048]{2,1,0:T(8,128)(2,1)S(1)} %bitcast.94), kind=kOutput, calls=%fused_computation.12 | convolution fusion | flops 17179869184 | bytes 33554432 | tf_op jit(solution)/shard_map/slcd,ldf->slcf/dot_general | solution.py:35
  137.1 20.0 %fusion.11 = f32[32,64,2048]{2,1,0:T(8,128)} fusion(bf16[32,64,2048]{2,1,0:T(8,128)(2,1)S(1)} %all_to_all.10, bf16[1,2048,2048]{2,1,0:T(8,128)(2,1)S(1)} %bitcast.96), kind=kOutput, calls=%fused_computation.14 | convolution fusion | flops 17179869184 | bytes 33554432 | tf_op jit(solution)/shard_map/slcd,ldf->slcf/dot_general | solution.py:34
  157.1 26.7 %fusion.14 = bf16[32,64,2048]{2,1,0:T(8,128)(2,1)} fusion(bf16[1,2048,2048]{2,1,0:T(8,128)(2,1)} %param.12, f32[32,64,2048]{2,1,0:T(8,128)} %fusion.9, f32[32,64,2048]{2,1,0:T(8,128)} %fusion.11), kind=kOutput, calls=%fused_computation.16 | convolution fusion | flops 17209229312 | bytes 50331648 | tf_op jit(solution)/shard_map/slcf,lfd->slcd/dot_general | solution.py:37
  183.8 6.6 %all-to-all-start.1 = ((bf16[32,64,2048]{2,1,0:T(8,128)(2,1)}), bf16[32,64,2048]{2,1,0:T(8,128)(2,1)}, u32[]{:S(2)}, u32[]{:S(2)}) async-start(bf16[32,64,2048]{2,1,0:T(8,128)(2,1)} %fusion.14), calls=%async_computation.1 | async-start | bytes 16777216 | tf_op jit(solution)/shard_map/all_to_all | solution.py:38
  190.5 0.6 fusion.35
  191.1 1.0 fusion.36
  192.2 111.6 %all-to-all-done.1 = bf16[32,64,2048]{2,1,0:T(8,128)(2,1)} async-done(((bf16[32,64,2048]{2,1,0:T(8,128)(2,1)}), bf16[32,64,2048]{2,1,0:T(8,128)(2,1)}, u32[]{:S(2)}, u32[]{:S(2)}) %all-to-all-start.1) | async-done | bytes 8388640 | tf_op jit(solution)/shard_map/all_to_all | solution.py:38
  303.8 8.4 %fusion.20 = f32[256,2048]{1,0:T(8,128)S(1)} fusion(bf16[32,64,2048]{2,1,0:T(8,128)(2,1)} %all-to-all-done.1, f32[256,2]{0,1:T(2,128)S(1)} %broadcast_divide_fusion, pred[256,2,64]{0,2,1:T(8,128)(4,1)S(1)} %copy-done.3, pred[256,2,32]{0,2,1:T(8,128)(4,1)S(1)} %copy-done.5), kind=kOutput, calls=%fused_computation.21 | convolution fusion | flops 4297588736 | bytes 10536960 | tf_op jit(solution)/shard_map/tkec,ecd->tkd/dot_general | solution.py:39
  312.2 2.5 add_convert_fusion
  (31 shorter events, 0.2 us)
Async XLA Ops:
  0.0 191.1 %copy-start = (f32[2048,32]{0,1:T(8,128)S(1)}, f32[2048,32]{0,1:T(8,128)}, u32[]{:S(2)}) copy-start(f32[2048,32]{0,1:T(8,128)} %param.8) | copy-start | bytes 786436
  1.9 115.3 %copy-start.4 = (pred[256,2,32]{0,2,1:T(8,128)(4,1)}, pred[256,2,32]{0,2,1:T(8,128)(4,1)S(1)}, u32[]{:S(2)}) copy-start(pred[256,2,32]{0,2,1:T(8,128)(4,1)S(1)} %iota_compare_fusion.3) | copy-start | bytes 49156
  3.7 0.6 copy-start.2
  4.8 112.3 %slice-start = ((s8[8388608]{0:T(1024)(128)(4,1)}), s8[4194304]{0:T(1024)(128)(4,1)S(1)}, s32[]{:S(2)}) async-start(s8[8388608]{0:T(1024)(128)(4,1)} %bitcast.93), calls=%async_computation.2 | async-start | bytes 8388608
  8.6 108.6 %slice-start.1 = ((s8[8388608]{0:T(1024)(128)(4,1)}), s8[4194304]{0:T(1024)(128)(4,1)S(1)}, s32[]{:S(2)}) async-start(s8[8388608]{0:T(1024)(128)(4,1)} %bitcast.93), calls=%async_computation.3 | async-start | bytes 8388608
  8.6 128.6 %slice-start.2 = ((s8[8388608]{0:T(1024)(128)(4,1)}), s8[4194304]{0:T(1024)(128)(4,1)S(1)}, s32[]{:S(2)}) async-start(s8[8388608]{0:T(1024)(128)(4,1)} %bitcast.95), calls=%async_computation.4 | async-start | bytes 8388608
  117.2 20.0 %slice-start.3 = ((s8[8388608]{0:T(1024)(128)(4,1)}), s8[4194304]{0:T(1024)(128)(4,1)S(1)}, s32[]{:S(2)}) async-start(s8[8388608]{0:T(1024)(128)(4,1)} %bitcast.95), calls=%async_computation.5 | async-start | bytes 8388608
  183.8 6.7 %copy-start.7 = (f32[2]{0:T(128)S(1)}, f32[2]{0:T(128)}, u32[]{:S(2)}) copy-start(f32[2]{0:T(128)} %param.13) | copy-start | bytes 28
  183.8 7.3 %copy-start.1 = (bf16[256,2048]{1,0:T(8,128)(2,1)S(1)}, bf16[256,2048]{1,0:T(8,128)(2,1)}, u32[]{:S(2)}) copy-start(bf16[256,2048]{1,0:T(8,128)(2,1)} %param.7) | copy-start | bytes 3145732
  183.8 8.4 %copy-start.6 = (s32[256,2]{0,1:T(2,128)S(1)}, s32[256,2]{0,1:T(2,128)}, u32[]{:S(2)}) copy-start(s32[256,2]{0,1:T(2,128)} %param.9) | copy-start | bytes 6148
  183.8 120.0 %copy-start.3 = (pred[256,2,64]{0,2,1:T(8,128)(4,1)S(1)}, pred[256,2,64]{0,2,1:T(8,128)(4,1)}, u32[]{:S(2)}) copy-start(pred[256,2,64]{0,2,1:T(8,128)(4,1)} %copy-done.2) | copy-start | bytes 98308
  183.8 120.0 %copy-start.5 = (pred[256,2,32]{0,2,1:T(8,128)(4,1)S(1)}, pred[256,2,32]{0,2,1:T(8,128)(4,1)}, u32[]{:S(2)}) copy-start(pred[256,2,32]{0,2,1:T(8,128)(4,1)} %copy-done.4) | copy-start | bytes 49156
  183.8 120.0 %all-to-all-start.1 = ((bf16[32,64,2048]{2,1,0:T(8,128)(2,1)}), bf16[32,64,2048]{2,1,0:T(8,128)(2,1)}, u32[]{:S(2)}, u32[]{:S(2)}) async-start(bf16[32,64,2048]{2,1,0:T(8,128)(2,1)} %fusion.14), calls=%async_computation.1 | async-start | bytes 16777216 | tf_op jit(solution)/shard_map/all_to_all | solution.py:38
where the time goes:
time: 315 us
  waiting for transfers between devices  112 us (36%)
  blocking collectives  109 us (35%)
  matrix products  79.7 us (25%)
  starting transfers between devices  6.65 us (2%)
  other arithmetic  5.16 us (2%)
    all_to_all x1, waiting for transfers between devices, local_step(): lax.all_to_all(expert_out.reshape(experts, capacity, model_width), 'ep',...  112 us
    all_to_all x1, blocking collectives, local_step(): lax.all_to_all(outgoing, 'ep', 0, 0, tiled=True)  109 us
    dot_general x1, matrix products, local_step(): jnp.einsum('slcf,lfd->slcd', middle, w_down, preferred_element_type=jnp.f...  26.7 us
    dot_general x1, matrix products, local_step(): jnp.einsum('slcd,ldf->slcf', incoming, w_up, preferred_element_type=jnp.f...  20 us
    dot_general x1, matrix products, local_step(): jnp.einsum('slcd,ldf->slcf', incoming, w_gate, preferred_element_type=jnp...  20 us
    dot_general x1, matrix products, local_step(): jnp.einsum('tkec,ecd->tkd', place.astype(jnp.bfloat16), returned, preferr...  8.36 us
    all_to_all x1, starting transfers between devices, local_step(): lax.all_to_all(expert_out.reshape(experts, capacity, model_width), 'ep',...  6.65 us
  transfers between devices with their start and end apart: 1, of which 1 were waited for; matrix products, arithmetic and copies ran while one was open for 1% of the time, Pallas kernels for 0%

commit v1 on v0

v1 whole, which is shorter than its diff:
```python
import functools
import jax
import jax.numpy as jnp
from jax import lax
from jax.experimental import pallas as pl
from jax.experimental.pallas import tpu as pltpu
from jax.sharding import PartitionSpec as P

MESH = pl.DeviceIdType.MESH
SIDE = 4

CODE = 0
GATHER = 3
CHUNK = 9
LEG = 17
BACK = 19
BLEG = 27
HOME = 29
HLEG = 61
NMSG = 69
SFWD = 69
SBFWD = 71
SLEG2 = 73
SHFWD = 74
SNBR = 82
SBACK = 86
SHOME = 93
NSEND = 117


def kernel_body(hid, code, code_col, gates, scale, w1h, w3h, w2h,
                out, fwd, back, bleg, hleg,
                w1, w3, w2, got, codes, pbuf, xs, outq, mid, ret, acc,
                send, recv, wsem, lsem):
    tokens, width = hid.shape
    cap = xs.shape[1] // SIDE
    ffn = w1.shape[1]
    half = tokens // 2
    tile = min(512, width)
    me = lax.axis_index('ep')
    y, x, c = lax.div(me, 2 * SIDE), lax.rem(lax.div(me, 2), SIDE), lax.rem(me, 2)

    def dev(yy, xx, cc):
        return (lax.rem(yy, SIDE) * SIDE + lax.rem(xx, SIDE)) * 2 + cc

    def qdev(o, core, axis):
        return dev(y + (1 - axis) * o, x + axis * o, core)

    def pdev(o):
        return dev(y + c * o, x + (1 - c) * o, c)

    def rcopy(src, dst, sid, rid, to):
        return pltpu.make_async_remote_copy(src_ref=src, dst_ref=dst, send_sem=send.at[sid], recv_sem=recv.at[rid], device_id={'ep': to}, device_id_type=MESH)

    sent = []

    def put(src, dst, sid, rid, to):
        cp = rcopy(src, dst, sid, rid, to)
        cp.start()
        sent.append((src, sid))

    def got_it(dst, rid):
        rcopy(dst, dst, 0, rid, me).wait_recv()

    lo, hi = pl.ds(0, half), pl.ds(half, half)

    for s, o in ((1, 1), (3, 3), (2, 2)):
        put(code, codes.at[s - 1], CODE + s - 1, CODE + s - 1, pdev(o))
    put(hid.at[lo], got.at[0, lo], GATHER + 0, GATHER + 0, pdev(1))
    put(hid.at[hi], got.at[2, hi], GATHER + 2, GATHER + 2, pdev(3))
    put(hid.at[hi], got.at[0, hi], GATHER + 1, GATHER + 1, pdev(1))
    put(hid.at[lo], got.at[2, lo], GATHER + 3, GATHER + 3, pdev(3))
    loads = [pltpu.make_async_copy(a, b, wsem.at[i]) for i, (a, b) in enumerate(((w1h, w1), (w3h, w3), (w2h, w2)))]
    for cp in loads:
        cp.start()

    order = (2, 1, 3, 0)

    def pack(s):
        cref = code if s == 0 else codes.at[s - 1]
        gref = hid if s == 0 else got.at[s - 1]
        c0, c1 = cref[0:1, :], cref[1:2, :]
        for i, o in enumerate(order):
            chip = lax.div(qdev(o, 0, c), 2)
            rows = lax.broadcasted_iota(jnp.int32, (2 * cap, tokens), 0) + chip * (2 * cap)
            hot = (rows == c0) | (rows == c1)
            pbuf[i * 2 * cap:(i + 1) * 2 * cap, :] = jnp.where(hot, 1.0, 0.0).astype(jnp.bfloat16)

        def one(t, carry):
            cols = pl.ds(pl.multiple_of(t * tile, tile), tile)
            r = jnp.dot(pbuf[...], gref[:, cols], preferred_element_type=jnp.float32).astype(jnp.bfloat16)
            dst = pl.ds(s * cap, cap)
            for i in range(6):
                outq[i, dst, cols] = r[i * cap:(i + 1) * cap]
            r0, r1 = r[6 * cap:7 * cap], r[7 * cap:8 * cap]
            own0 = c == 0
            xs[0, dst, cols] = jnp.where(own0, r0, r1)
            outq[6, dst, cols] = jnp.where(own0, r1, r0)
            return carry

        lax.fori_loop(0, width // tile, one, 0)

    pack(0)
    got_it(got.at[0, lo], GATHER + 0)
    put(got.at[0, lo], got.at[1, lo], GATHER + 4, GATHER + 4, pdev(1))
    got_it(got.at[2, hi], GATHER + 2)
    put(got.at[2, hi], got.at[1, hi], GATHER + 5, GATHER + 5, pdev(3))
    got_it(codes.at[0], CODE + 0)
    got_it(got.at[0, hi], GATHER + 1)
    pack(1)
    got_it(codes.at[2], CODE + 2)
    got_it(got.at[2, lo], GATHER + 3)
    pack(3)
    got_it(codes.at[1], CODE + 1)
    got_it(got.at[1, lo], GATHER + 4)
    got_it(got.at[1, hi], GATHER + 5)
    pack(2)

    put(outq.at[0], fwd.at[0], LEG + 0, LEG + 0, qdev(1, c, c))
    put(outq.at[1], fwd.at[1], LEG + 1, LEG + 1, qdev(3, c, c))
    put(outq.at[2], xs.at[2 + c], SNBR + 0, CHUNK + 2 + c, qdev(1, 0, c))
    put(outq.at[5], xs.at[2 + c], SNBR + 1, CHUNK + 2 + c, qdev(3, 1, c))
    put(outq.at[6], xs.at[1], CHUNK + 1, CHUNK + 1, qdev(0, 1 - c, c))
    put(outq.at[3], xs.at[6 + c], SNBR + 2, CHUNK + 6 + c, qdev(1, 1, c))
    put(outq.at[4], xs.at[6 + c], SNBR + 3, CHUNK + 6 + c, qdev(3, 0, c))

    def chunk_forward():
        got_it(fwd.at[0], LEG + 0)
        put(fwd.at[0], xs.at[4 + c], SFWD + 0, CHUNK + 4 + c, qdev(1, 0, c))
        got_it(fwd.at[1], LEG + 1)
        put(fwd.at[1], xs.at[4 + c], SFWD + 1, CHUNK + 4 + c, qdev(3, 1, c))

    locals_ = []

    def part(s):
        return pl.ds(s * cap, cap)

    def home(ref, blk, k, n):
        put(ref.at[part(1)], ret.at[8 + blk], SHOME + 3 * n, HOME + 8 + blk, pdev(3))
        put(ref.at[part(3)], ret.at[24 + blk], SHOME + 3 * n + 1, HOME + 24 + blk, pdev(1))
        put(ref.at[part(2)], hleg.at[blk], SHOME + 3 * n + 2, HLEG + blk, pdev(1 + 2 * k))

    def home_from(blk, k, n):
        got_it(back.at[blk], BACK + blk)
        home(back.at[blk], blk, k, n)
        cp = pltpu.make_async_copy(back.at[blk, part(0)], ret.at[blk], lsem.at[n])
        cp.start()
        locals_.append((blk, n))

    def home_forward(blk, n):
        got_it(hleg.at[blk], HLEG + blk)
        put(hleg.at[blk], ret.at[16 + blk], SHFWD + n, HOME + 16 + blk, pdev(1 + 2 * (blk % 2)))

    def back_forward():
        got_it(bleg.at[0], BLEG + 0)
        put(bleg.at[0], back.at[4], SBFWD + 0, BACK + 4, qdev(1, c, c))
        got_it(bleg.at[1], BLEG + 1)
        put(bleg.at[1], back.at[5], SBFWD + 1, BACK + 5, qdev(3, c, c))

    def after(step):
        if step == 0:
            ret[c] = xs[0, part(0), :]
            home(xs.at[0], c, c, 0)
        elif step == 1:
            put(xs.at[1], back.at[c], SBACK + 0, BACK + c, qdev(0, 1 - c, c))
            chunk_forward()
        elif step in (2, 3):
            put(xs.at[step], back.at[2 + 5 * c], SBACK + step - 1, BACK + 2 + 5 * c, qdev(3 + 2 * c, step % 2, step % 2))
            if step == 3:
                home_from(1 - c, 1 - c, 1)
        elif step in (4, 5):
            put(xs.at[step], bleg.at[c], SBACK + step - 1, BLEG + c, qdev(1 + 2 * c, step % 2, step % 2))
            if step == 5:
                for k in range(2):
                    home_forward(k, k)
        else:
            put(xs.at[step], back.at[6 - 3 * c], SBACK + step - 1, BACK + 6 - 3 * c, qdev(1 + 2 * c, step % 2, step % 2))

    for cp in loads:
        cp.wait()

    def expert(step):
        def up(t, carry):
            cols = pl.ds(pl.multiple_of(t * ftile, ftile), ftile)
            a = jnp.dot(xs[step], w1[:, cols], preferred_element_type=jnp.float32)
            b = jnp.dot(xs[step], w3[:, cols], preferred_element_type=jnp.float32)
            mid[:, cols] = (jax.nn.silu(a) * b).astype(jnp.bfloat16)
            return carry

        def down(t, carry):
            cols = pl.ds(pl.multiple_of(t * tile, tile), tile)
            xs[step, :, cols] = jnp.dot(mid[...], w2[:, cols], preferred_element_type=jnp.float32).astype(jnp.bfloat16)
            return carry

        ftile = min(512, ffn)
        lax.fori_loop(0, ffn // ftile, up, 0)
        lax.fori_loop(0, width // tile, down, 0)

    def step_body(step, carry):
        @pl.when(step > 0)
        def _():
            got_it(xs.at[step], CHUNK + step)
        expert(step)
        for j in range(8):
            @pl.when(step == j)
            def _(j=j):
                after(j)
        return carry

    for j in range(8):
        if j: got_it(xs.at[j], CHUNK + j)
        expert(j)
        after(j)

    home_from(2, 0, 2)
    home_from(7, 1, 3)
    back_forward()
    home_from(6, 0, 4)
    home_from(3, 1, 5)
    home_forward(2, 2)
    home_forward(7, 3)
    home_from(4, 0, 6)
    home_from(5, 1, 7)
    home_forward(6, 4)
    home_forward(3, 5)
    home_forward(4, 6)
    home_forward(5, 7)

    def combine(s, first):
        r = lax.broadcasted_iota(jnp.int32, (tokens, 8 * cap), 1) + s * 8 * cap
        h0 = jnp.where(code_col[:, 0:1] == r, 1.0, 0.0).astype(jnp.bfloat16)
        h1 = jnp.where(code_col[:, 1:2] == r, 1.0, 0.0).astype(jnp.bfloat16)
        g0, g1 = gates[:, 0:1], gates[:, 1:2]
        for t in range(width // tile):
            cols = pl.ds(t * tile, tile)
            rows = ret[s * 8:(s + 1) * 8, :, cols].reshape(8 * cap, tile)
            v = g0 * jnp.dot(h0, rows, preferred_element_type=jnp.float32) + g1 * jnp.dot(h1, rows, preferred_element_type=jnp.float32)
            if first:
                acc[:, cols] = v
            else:
                acc[:, cols] += v

    for blk, n in locals_:
        pltpu.make_async_copy(back.at[blk, part(0)], ret.at[blk], lsem.at[n]).wait()
    combine(0, True)
    for s in (1, 3, 2):
        for blk in range(8):
            got_it(ret.at[s * 8 + blk], HOME + s * 8 + blk)
        combine(s, False)
    for t in range(width // tile):
        cols = pl.ds(t * tile, tile)
        out[:, cols] = (scale[0] * hid[:, cols].astype(jnp.float32) + scale[1] * acc[:, cols]).astype(out.dtype)
    for src, sid in sent:
        rcopy(src, src, sid, 0, me).wait_send()


def fused(hidden, code, code_col, gates, scale, w1, w3, w2, cap):
    tokens, width = hidden.shape
    ffn = w1.shape[1]
    rows = SIDE * cap
    bf = jnp.bfloat16
    vm = pl.BlockSpec(memory_space=pltpu.VMEM)
    hbm = pl.BlockSpec(memory_space=pl.ANY)
    return pl.pallas_call(
        kernel_body,
        out_shape=[
            jax.ShapeDtypeStruct((tokens, width), bf),
            jax.ShapeDtypeStruct((2, rows, width), bf),
            jax.ShapeDtypeStruct((8, rows, width), bf),
            jax.ShapeDtypeStruct((2, rows, width), bf),
            jax.ShapeDtypeStruct((8, cap, width), bf),
        ],
        in_specs=[vm, vm, vm, vm, pl.BlockSpec(memory_space=pltpu.SMEM), hbm, hbm, hbm],
        out_specs=[vm, hbm, hbm, hbm, hbm],
        scratch_shapes=[
            pltpu.VMEM((width, ffn), bf), pltpu.VMEM((width, ffn), bf), pltpu.VMEM((ffn, width), bf),
            pltpu.VMEM((3, tokens, width), bf),
            pltpu.VMEM((3,) + code.shape, jnp.int32),
            pltpu.VMEM((8 * cap, tokens), bf),
            pltpu.VMEM((8, rows, width), bf),
            pltpu.VMEM((7, rows, width), bf),
            pltpu.VMEM((rows, ffn), bf),
            pltpu.VMEM((32, cap, width), bf),
            pltpu.VMEM((tokens, width), jnp.float32),
            pltpu.SemaphoreType.DMA((NSEND,)),
            pltpu.SemaphoreType.DMA((NMSG,)),
            pltpu.SemaphoreType.DMA((3,)),
            pltpu.SemaphoreType.DMA((8,)),
        ],
        compiler_params=pltpu.CompilerParams(has_side_effects=True, vmem_limit_bytes=67043328),
        name='moe',
    )(hidden, code, code_col, gates, scale, w1, w3, w2)[0]


def route(hidden, router_w, expert_ids, experts, cap):
    tokens, choices = expert_ids.shape
    logits = jnp.dot(hidden.astype(jnp.float32), router_w, precision=lax.Precision.HIGHEST, preferred_element_type=jnp.float32)
    prob = jax.nn.softmax(logits, axis=-1)
    pick = expert_ids[:, :, None] == jnp.arange(experts, dtype=jnp.int32)[None, None, :]
    picked = jnp.sum(jnp.where(pick, prob[:, None, :], 0.0), axis=-1)
    gates = picked / jnp.sum(picked, axis=1, keepdims=True)
    hot = pick.reshape(tokens * choices, experts).astype(jnp.int32)
    earlier = jnp.cumsum(hot, axis=0) - hot
    slot = jnp.sum(earlier * hot, axis=1).reshape(tokens, choices)
    code = expert_ids * cap + slot
    me = lax.axis_index('ep')
    y, x, c = me // (2 * SIDE), (me // 2) % SIDE, me % 2
    ey, ex, ek = expert_ids // (2 * SIDE), (expert_ids // 2) % SIDE, expert_ids % 2
    dy, dx = (ey - y) % SIDE, (ex - x) % SIDE
    dp, dq = jnp.where(c == 0, dx, dy), jnp.where(c == 0, dy, dx)
    code_col = ((dp * SIDE + dq) * 2 + ek) * cap + slot
    return gates, code, code_col


def solution(mesh):
    ep_size = mesh.shape['ep']

    def local_step(hidden, router_w, expert_ids, w_gate, w_up, w_down, post_scale):
        tokens = hidden.shape[0]
        experts = w_gate.shape[0] * ep_size
        cap = tokens // max(1, experts // 8)
        gates, code, code_col = route(hidden, router_w, expert_ids, experts, cap)
        code_rows = jnp.concatenate([code.T, jnp.zeros((6, tokens), jnp.int32)], axis=0)
        return fused(hidden, code_rows, code_col, gates, post_scale, w_gate[0], w_up[0], w_down[0], cap)

    tok_spec = P(('dp', 'ep'))
    return jax.shard_map(local_step, mesh=mesh, in_specs=(tok_spec, P(), tok_spec, P('ep'), P('ep'), P('ep'), P()), out_specs=tok_spec, check_vma=False)
```

time: 315 us -> 200 us (0.63)
  the two profiles are of different devices: /device:TPU:103 before, /device:TPU:98 now
where the time goes in v1:
time: 200 us
  Pallas kernels  187 us (94%)
  other arithmetic  5.25 us (3%)
  local copies, waits for them, and re-layouts  4.75 us (2%)
  matrix products  2.3 us (1%)
    pallas_call x1, Pallas kernels, fused(): pl.pallas_call(kernel_body, out_shape=[jax.ShapeDtypeStruct((tokens, widt...  187 us

profile of v1, /device:TPU:98, one launch (start us, length us, event | category | flops | bytes accessed | tf_op | source)
XLA Modules:
  0.0 199.5 jit_solution(8492895134462230960)
XLA Ops:
  0.0 0.7 broadcast_compare_fusion
  0.7 0.2 copy.64
  0.9 2.3 %fusion.17 = (f32[256]{0:T(256)S(1)}, f32[256,32]{0,1:T(8,128)S(1)}) fusion(bf16[256,2048]{1,0:T(8,128)(2,1)} %hid.1, f32[2048,32]{0,1:T(8,128)} %param.8), kind=kOutput, calls=%fused_computation.47 | convolution fusion | flops 201334528 | bytes 1344512 | tf_op jit(solution)/shard_map/dot_general | solution.py:297
  3.2 0.7 select_reduce_fusion
  3.9 0.8 copy.55
  4.8 0.1 eq.48
  4.9 0.1 eq.44
  5.1 1.2 reduce-window.6
  6.2 0.2 slice_reduce_fusion
  6.5 0.1 fusion.13
  6.6 0.1 reshape.26
  6.8 1.0 fusion.8.code_col
  7.8 0.1 copy.58
  7.9 0.7 add_bitcast_fusion.1
  8.5 0.6 concatenate.3.code
  9.1 0.1 copy.69
  9.3 0.8 broadcast_divide_fusion.gates
  10.0 187.2 %moe.1 = (bf16[256,2048]{1,0:T(8,128)(2,1)}, bf16[2,256,2048]{2,1,0:T(8,128)(2,1)}, bf16[8,256,2048]{2,1,0:T(8,128)(2,1)}, bf16[2,256,2048]{2,1,0:T(8,128)(2,1)}, bf16[8,64,2048]{2,1,0:T(8,128)(2,1)}) custom-call(bf16[256,2048]{1,0:T(8,128)(2,1)} %hid.1, s32[8,256]{1,0:T(8,128)} %concatenate.3.code, s32[256,2]{1,0:T(8,128)} %fusion.8.code_col, ...), custom_call_target="tpu_custom_call" | custom-call | tf_op jit(solution)/shard_map/moe/pallas_call | solution.py:264
  197.2 2.3 %copy.86 = bf16[256,2048]{1,0:T(8,128)(2,1)} copy(bf16[256,2048]{1,0:T(8,128)(2,1)} %get-tuple-element.6) | data formatting | bytes 2097152
  (5 shorter events, 0.1 us)

commit v2 on v1

v2 whole, which is shorter than its diff:
```python
import functools
import jax
import jax.numpy as jnp
from jax import lax
from jax.experimental import pallas as pl
from jax.experimental.pallas import tpu as pltpu
from jax.sharding import PartitionSpec as P

MESH = pl.DeviceIdType.MESH
SIDE = 4

CODE = 0
GATHER = 3
CHUNK = 9
LEG = 17
BACK = 19
BLEG = 27
HOPP = 29
HOME = 33
NMSG = 39
SFWD = 39
SBFWD = 41
SNBR = 43
SBACK = 47
NSEND = 54
LHID, LRW, LW1, LW3, LW2, LOUT = 0, 1, 2, 3, 4, 5


def kernel_body(ids, idst, scale, hidh, rwh, w1h, w3h, w2h,
                out, fwd, bleg,
                hid, rw, w1, w3, w2, got, code, codes, gate, pbuf, xs, outq, mid, back, lbuf, rbuf,
                send, recv, lsem):
    tokens, width = hid.shape
    cap = xs.shape[1] // SIDE
    ffn = w1.shape[1]
    experts = rw.shape[1]
    half = tokens // 2
    tile = min(512, width)
    ftile = min(512, ffn)
    f32, bf16 = jnp.float32, jnp.bfloat16
    me = lax.axis_index('ep')
    y, x, c = lax.div(me, 2 * SIDE), lax.rem(lax.div(me, 2), SIDE), lax.rem(me, 2)

    def dev(yy, xx, cc):
        return (lax.rem(yy, SIDE) * SIDE + lax.rem(xx, SIDE)) * 2 + cc

    def qdev(o, core, axis):
        return dev(y + (1 - axis) * o, x + axis * o, core)

    def pdev(o):
        return dev(y + c * o, x + (1 - c) * o, c)

    def rcopy(src, dst, sid, rid, to):
        return pltpu.make_async_remote_copy(src_ref=src, dst_ref=dst, send_sem=send.at[sid], recv_sem=recv.at[rid], device_id={'ep': to}, device_id_type=MESH)

    sent = []

    def put(src, dst, sid, rid, to):
        cp = rcopy(src, dst, sid, rid, to)
        cp.start()
        sent.append((src, sid))

    def drain():
        while sent:
            src, sid = sent.pop(0)
            rcopy(src, src, sid, 0, me).wait_send()

    def got_it(dst, rid):
        rcopy(dst, dst, 0, rid, me).wait_recv()

    def fetch(src, dst, n):
        cp = pltpu.make_async_copy(src, dst, lsem.at[n])
        cp.start()
        return cp

    lo, hi = pl.ds(0, half), pl.ds(half, half)

    barrier = pltpu.get_barrier_semaphore()
    peers = [pdev(1), pdev(2), pdev(3), qdev(0, 1 - c, c)]
    peers += [qdev(o, k, c) for o in (1, 3) for k in range(2)]
    peers += [qdev(o, 1 - c, 1 - c) for o in (1, 3)]
    for to in peers:
        pl.semaphore_signal(barrier, inc=1, device_id={'ep': to}, device_id_type=MESH)
    load_hid = fetch(hidh, hid, LHID)
    load_rw = fetch(rwh, rw, LRW)
    pl.semaphore_wait(barrier, len(peers))

    put(hidh.at[lo], got.at[0, lo], GATHER + 0, GATHER + 0, pdev(1))
    put(hidh.at[hi], got.at[2, hi], GATHER + 2, GATHER + 2, pdev(3))
    put(hidh.at[hi], got.at[0, hi], GATHER + 1, GATHER + 1, pdev(1))
    put(hidh.at[lo], got.at[2, lo], GATHER + 3, GATHER + 3, pdev(3))
    loads = [fetch(w1h, w1, LW1), fetch(w3h, w3, LW3), fetch(w2h, w2, LW2)]

    erow = lax.broadcasted_iota(jnp.int32, (experts, tokens), 0)
    hot0, hot1 = idst[0:1, :] == erow, idst[1:2, :] == erow
    one0, one1 = jnp.where(hot0, 1.0, 0.0), jnp.where(hot1, 1.0, 0.0)
    earlier = lax.broadcasted_iota(jnp.int32, (tokens, tokens), 0) < lax.broadcasted_iota(jnp.int32, (tokens, tokens), 1)
    upper = jnp.where(earlier, 1.0, 0.0).astype(bf16)
    before0 = jnp.dot(one0.astype(bf16), upper, preferred_element_type=f32)
    before1 = jnp.dot(one1.astype(bf16), upper, preferred_element_type=f32) + jnp.sum(one0, axis=1, keepdims=True)
    slot0 = jnp.sum(jnp.where(hot0, before0, 0.0), axis=0, keepdims=True)
    slot1 = jnp.sum(jnp.where(hot1, before1, 0.0), axis=0, keepdims=True)
    code[...] = jnp.zeros(code.shape, jnp.int32)
    code[0:1, :] = idst[0:1, :] * cap + slot0.astype(jnp.int32)
    code[1:2, :] = idst[1:2, :] * cap + slot1.astype(jnp.int32)

    order = (2, 1, 3, 0)

    def code_rows(s):
        return code if s == 0 else codes.at[s - 1]

    def slots(o):
        return lax.broadcasted_iota(jnp.int32, (2 * cap, tokens), 0) + qdev(o, 0, c) * cap

    def pack(s):
        cref = code_rows(s)
        gref = hid if s == 0 else got.at[s - 1]
        c0, c1 = cref[0:1, :], cref[1:2, :]
        for i, o in enumerate(order):
            rows = slots(o)
            pbuf[i * 2 * cap:(i + 1) * 2 * cap, :] = jnp.where((rows == c0) | (rows == c1), 1.0, 0.0).astype(bf16)

        def one(t, carry):
            cols = pl.ds(pl.multiple_of(t * tile, tile), tile)
            r = jnp.dot(pbuf[...], gref[:, cols], preferred_element_type=f32).astype(bf16)
            dst = pl.ds(s * cap, cap)
            for i in range(6):
                outq[i, dst, cols] = r[i * cap:(i + 1) * cap]
            r0, r1 = r[6 * cap:7 * cap], r[7 * cap:8 * cap]
            own0 = c == 0
            xs[0, dst, cols] = jnp.where(own0, r0, r1)
            outq[6, dst, cols] = jnp.where(own0, r1, r0)
            return carry

        lax.fori_loop(0, width // tile, one, 0)

    load_hid.wait()
    pack(0)
    for s, o in ((1, 1), (3, 3), (2, 2)):
        put(code, codes.at[s - 1], CODE + s - 1, CODE + s - 1, pdev(o))
    got_it(got.at[0, lo], GATHER + 0)
    put(got.at[0, lo], got.at[1, lo], GATHER + 4, GATHER + 4, pdev(1))
    got_it(got.at[2, hi], GATHER + 2)
    put(got.at[2, hi], got.at[1, hi], GATHER + 5, GATHER + 5, pdev(3))

    load_rw.wait()
    w = rw[...]
    wa = w.astype(bf16)
    w = w - wa.astype(f32)
    wb = w.astype(bf16)
    wc = (w - wb.astype(f32)).astype(bf16)
    logits = jnp.dot(hid[...], wc, preferred_element_type=f32) + jnp.dot(hid[...], wb, preferred_element_type=f32)
    logits = logits + jnp.dot(hid[...], wa, preferred_element_type=f32)
    ex = jnp.exp(logits - jnp.max(logits, axis=1, keepdims=True))
    prob = ex / jnp.sum(ex, axis=1, keepdims=True)
    ecol = lax.broadcasted_iota(jnp.int32, (tokens, experts), 1)
    p0 = jnp.sum(jnp.where(ids[:, 0:1] == ecol, prob, 0.0), axis=1, keepdims=True)
    p1 = jnp.sum(jnp.where(ids[:, 1:2] == ecol, prob, 0.0), axis=1, keepdims=True)
    gate[0] = jnp.broadcast_to(p0 / (p0 + p1), gate.shape[1:])
    gate[1] = jnp.broadcast_to(p1 / (p0 + p1), gate.shape[1:])

    got_it(codes.at[0], CODE + 0)
    got_it(got.at[0, hi], GATHER + 1)
    pack(1)
    got_it(codes.at[2], CODE + 2)
    got_it(got.at[2, lo], GATHER + 3)
    pack(3)
    got_it(codes.at[1], CODE + 1)
    got_it(got.at[1, lo], GATHER + 4)
    got_it(got.at[1, hi], GATHER + 5)
    pack(2)

    put(outq.at[0], fwd.at[0], LEG + 0, LEG + 0, qdev(1, c, c))
    put(outq.at[1], fwd.at[1], LEG + 1, LEG + 1, qdev(3, c, c))
    put(outq.at[2], xs.at[2 + c], SNBR + 0, CHUNK + 2 + c, qdev(1, 0, c))
    put(outq.at[5], xs.at[2 + c], SNBR + 1, CHUNK + 2 + c, qdev(3, 1, c))
    put(outq.at[6], xs.at[1], CHUNK + 1, CHUNK + 1, qdev(0, 1 - c, c))

    def chunk_forward():
        got_it(fwd.at[0], LEG + 0)
        put(fwd.at[0], xs.at[4 + c], SFWD + 0, CHUNK + 4 + c, qdev(1, 0, c))
        got_it(fwd.at[1], LEG + 1)
        put(fwd.at[1], xs.at[4 + c], SFWD + 1, CHUNK + 4 + c, qdev(3, 1, c))
        put(outq.at[3], xs.at[6 + c], SNBR + 2, CHUNK + 6 + c, qdev(1, 1, c))
        put(outq.at[4], xs.at[6 + c], SNBR + 3, CHUNK + 6 + c, qdev(3, 0, c))

    def back_forward():
        got_it(bleg.at[0], BLEG + 0)
        put(bleg.at[0], back.at[4], SBFWD + 0, BACK + 4, qdev(1, c, c))
        got_it(bleg.at[1], BLEG + 1)
        put(bleg.at[1], back.at[5], SBFWD + 1, BACK + 5, qdev(3, c, c))

    def after(step):
        k = step % 2
        if step == 1:
            put(xs.at[1], back.at[c], SBACK + 0, BACK + c, qdev(0, 1 - c, c))
            chunk_forward()
        elif step in (2, 3):
            put(xs.at[step], back.at[2 + 5 * c], SBACK + step - 1, BACK + 2 + 5 * c, qdev(3 + 2 * c, k, k))
        elif step in (4, 5):
            put(xs.at[step], bleg.at[c], SBACK + step - 1, BLEG + c, qdev(1 + 2 * c, k, k))
        else:
            put(xs.at[step], back.at[6 - 3 * c], SBACK + step - 1, BACK + 6 - 3 * c, qdev(1 + 2 * c, k, k))
            if step == 6:
                back_forward()

    for cp in loads:
        cp.wait()

    def expert(step):
        def up(t, carry):
            cols = pl.ds(pl.multiple_of(t * ftile, ftile), ftile)
            a = jnp.dot(xs[step], w1[:, cols], preferred_element_type=f32)
            b = jnp.dot(xs[step], w3[:, cols], preferred_element_type=f32)
            mid[:, cols] = (jax.nn.silu(a) * b).astype(bf16)
            return carry

        def down(t, carry):
            cols = pl.ds(pl.multiple_of(t * tile, tile), tile)
            r = jnp.dot(mid[...], w2[:, cols], preferred_element_type=f32).astype(bf16)
            if step == 0:
                back[c, :, cols] = r
            else:
                xs[step, :, cols] = r
            return carry

        lax.fori_loop(0, ffn // ftile, up, 0)
        lax.fori_loop(0, width // tile, down, 0)

    for step in range(8):
        if step:
            got_it(xs.at[step], CHUNK + step)
        expert(step)
        if step:
            after(step)

    drain()

    def place(s, k, dst):
        ck = code_rows(s)[k:k + 1, :]
        for o in range(SIDE):
            pbuf[o * 2 * cap:(o + 1) * 2 * cap, :] = jnp.where(slots(o) == ck, 1.0, 0.0).astype(bf16)

        def one(t, carry):
            cols = pl.ds(pl.multiple_of(t * tile, tile), tile)
            rows = back[:, pl.ds(s * cap, cap), cols].reshape(8 * cap, tile)
            dst[:, cols] = lax.dot_general(pbuf[...], rows, (((0,), (0,)), ((), ())), preferred_element_type=f32).astype(bf16)
            return carry

        lax.fori_loop(0, width // tile, one, 0)

    got_it(back.at[1 - c], BACK + 1 - c)
    for blk in (2, 7, 3, 6, 4, 5):
        got_it(back.at[blk], BACK + blk)
    place(2, 0, outq.at[0])
    for i, h in enumerate((lo, hi)):
        put(outq.at[0, h], lbuf.at[0, h], HOPP + i, HOPP + i, pdev(1))
    place(2, 1, outq.at[1])
    for i, h in enumerate((lo, hi)):
        put(outq.at[1, h], lbuf.at[1, h], HOPP + 2 + i, HOPP + 2 + i, pdev(3))
    place(3, 1, outq.at[2])
    put(outq.at[2], rbuf.at[1], HOME + 0, HOME + 0, pdev(1))
    place(1, 0, outq.at[3])
    put(outq.at[3], rbuf.at[2], HOME + 1, HOME + 1, pdev(3))
    place(3, 0, outq.at[4])
    place(1, 1, outq.at[5])
    for i, h in enumerate((lo, hi)):
        got_it(lbuf.at[0, h], HOPP + i)
        outq[4, h, :] = outq[4, h, :] + lbuf[0, h, :]
        put(outq.at[4, h], rbuf.at[0, h], HOME + 2 + i, HOME + 2 + i, pdev(1))
        got_it(lbuf.at[1, h], HOPP + 2 + i)
        outq[5, h, :] = outq[5, h, :] + lbuf[1, h, :]
        put(outq.at[5, h], rbuf.at[3, h], HOME + 4 + i, HOME + 4 + i, pdev(3))
    place(0, 0, got.at[0])
    place(0, 1, got.at[1])
    got_it(rbuf.at[1], HOME + 0)
    got_it(rbuf.at[2], HOME + 1)
    step_rows = min(64, half)
    outs = []
    for i, h in enumerate((lo, hi)):
        got_it(rbuf.at[0, h], HOME + 2 + i)
        got_it(rbuf.at[3, h], HOME + 4 + i)

        def finish(j, carry):
            r = pl.ds(pl.multiple_of(i * half + j * step_rows, step_rows), step_rows)
            g0, g1 = gate[0, r, 0:1], gate[1, r, 0:1]
            for t in range(width // tile):
                cols = pl.ds(t * tile, tile)
                y0 = (got[0, r, cols] + rbuf[0, r, cols] + rbuf[2, r, cols]).astype(f32)
                y1 = (got[1, r, cols] + rbuf[1, r, cols] + rbuf[3, r, cols]).astype(f32)
                mixed = g0 * y0 + g1 * y1
                outq[6, r, cols] = (scale[0] * hid[r, cols].astype(f32) + scale[1] * mixed).astype(bf16)
            return carry

        lax.fori_loop(0, half // step_rows, finish, 0)
        outs.append(fetch(outq.at[6, h], out.at[h], LOUT + i))
    drain()
    for cp in outs:
        cp.wait()


def fused(hidden, rw, ids, idst, scale, w1, w3, w2, cap):
    tokens, width = hidden.shape
    ffn = w1.shape[1]
    rows = SIDE * cap
    bf = jnp.bfloat16
    vm = pl.BlockSpec(memory_space=pltpu.VMEM)
    hbm = pl.BlockSpec(memory_space=pl.ANY)
    return pl.pallas_call(
        kernel_body,
        out_shape=[
            jax.ShapeDtypeStruct((tokens, width), bf),
            jax.ShapeDtypeStruct((2, rows, width), bf),
            jax.ShapeDtypeStruct((2, rows, width), bf),
        ],
        in_specs=[vm, vm, pl.BlockSpec(memory_space=pltpu.SMEM), hbm, hbm, hbm, hbm, hbm],
        out_specs=[hbm, hbm, hbm],
        scratch_shapes=[
            pltpu.VMEM((tokens, width), bf),
            pltpu.VMEM(rw.shape, jnp.float32),
            pltpu.VMEM((width, ffn), bf), pltpu.VMEM((width, ffn), bf), pltpu.VMEM((ffn, width), bf),
            pltpu.VMEM((3, tokens, width), bf),
            pltpu.VMEM(idst.shape, jnp.int32),
            pltpu.VMEM((3,) + idst.shape, jnp.int32),
            pltpu.VMEM((2, tokens, 128), jnp.float32),
            pltpu.VMEM((8 * cap, tokens), bf),
            pltpu.VMEM((8, rows, width), bf),
            pltpu.VMEM((7, rows, width), bf),
            pltpu.VMEM((rows, ffn), bf),
            pltpu.VMEM((8, rows, width), bf),
            pltpu.VMEM((2, tokens, width), bf),
            pltpu.VMEM((4, tokens, width), bf),
            pltpu.SemaphoreType.DMA((NSEND,)),
            pltpu.SemaphoreType.DMA((NMSG,)),
            pltpu.SemaphoreType.DMA((7,)),
        ],
        compiler_params=pltpu.CompilerParams(has_side_effects=True, collective_id=0, vmem_limit_bytes=67043328),
        name='moe',
    )(ids, idst, scale, hidden, rw, w1, w3, w2)[0]


def solution(mesh):
    ep_size = mesh.shape['ep']

    def local_step(hidden, router_w, expert_ids, w_gate, w_up, w_down, post_scale):
        tokens = hidden.shape[0]
        experts = w_gate.shape[0] * ep_size
        cap = tokens // max(1, experts // 8)
        idst = jnp.pad(expert_ids.T, ((0, 6), (0, 0)))
        return fused(hidden, router_w, expert_ids, idst, post_scale, w_gate[0], w_up[0], w_down[0], cap)

    tok_spec = P(('dp', 'ep'))
    return jax.shard_map(local_step, mesh=mesh, in_specs=(tok_spec, P(), tok_spec, P('ep'), P('ep'), P('ep'), P()), out_specs=tok_spec, check_vma=False)
```

time: 200 us -> 172 us (0.86)
  the two profiles are of different devices: /device:TPU:98 before, /device:TPU:97 now
where the time goes in v2:
time: 172 us
  Pallas kernels  165 us (96%)
  local copies, waits for them, and re-layouts  7.31 us (4%)
    pallas_call x1, Pallas kernels, fused(): pl.pallas_call(kernel_body, out_shape=[jax.ShapeDtypeStruct((tokens, widt...  165 us
    unnamed x3, local copies, waits for them, and re-layouts  6.03 us

profile of v2, /device:TPU:97, one launch (start us, length us, event | category | flops | bytes accessed | tf_op | source)
XLA Modules:
  0.0 172.0 jit_solution(9608262559924034275)
XLA Ops:
  0.0 1.3 pad.4.idst
  1.3 1.5 copy.8.ids
  2.7 2.3 %copy.9.rwh = f32[2048,32]{1,0:T(8,128)} copy(f32[2048,32]{0,1:T(8,128)} %param.8) | data formatting | bytes 524288 | tf_op args[1]
  5.0 164.7 %moe.1 = (bf16[256,2048]{1,0:T(8,128)(2,1)}, bf16[2,256,2048]{2,1,0:T(8,128)(2,1)}, bf16[2,256,2048]{2,1,0:T(8,128)(2,1)}) custom-call(s32[256,2]{1,0:T(8,128)} %copy.8.ids, s32[8,256]{1,0:T(8,128)} %pad.4.idst, f32[2]{0:T(128)} %scale.1, bf16[256,2048]{1,0:T(8,128)(2,1)} %hidh.1, f32[2048,32]{1,0:T(8,128)} %copy.9.rwh, bf16[2048,2048]{1,0:T(8,128)(2,1)} %bitcast.4, ...), custom_call_target="tpu_custom_call" | custom-call | tf_op jit(solution)/shard_map/moe/pallas_call | solution.py:309
  169.7 2.3 %copy.11 = bf16[256,2048]{1,0:T(8,128)(2,1)} copy(bf16[256,2048]{1,0:T(8,128)(2,1)} %get-tuple-element.6) | data formatting | bytes 2097152

commit v3 on v2

--- a/solution.py
+++ b/solution.py
@@ -13,27 +13,27 @@
 GATHER = 3
 CHUNK = 9
 LEG = 17
-BACK = 19
-BLEG = 27
-HOPP = 29
-HOME = 33
-NMSG = 39
-SFWD = 39
-SBFWD = 41
-SNBR = 43
-SBACK = 47
-NSEND = 54
+BACK = 21
+BLEG = 29
+HOPP = 31
+HOME = 35
+NMSG = 41
+SFWD = 41
+SBFWD = 43
+SNBR = 45
+SBACK = 49
+NSEND = 56
 LHID, LRW, LW1, LW3, LW2, LOUT = 0, 1, 2, 3, 4, 5
 
 
-def kernel_body(ids, idst, scale, hidh, rwh, w1h, w3h, w2h,
+def kernel_body(idst, scale, hidh, rwh, w1h, w3h, w2h,
                 out, fwd, bleg,
                 hid, rw, w1, w3, w2, got, code, codes, gate, pbuf, xs, outq, mid, back, lbuf, rbuf,
                 send, recv, lsem):
     tokens, width = hid.shape
     cap = xs.shape[1] // SIDE
     ffn = w1.shape[1]
-    experts = rw.shape[1]
+    experts = rw.shape[0]
     half = tokens // 2
     tile = min(512, width)
     ftile = min(512, ffn)
@@ -74,6 +74,10 @@
         return cp
 
     lo, hi = pl.ds(0, half), pl.ds(half, half)
+    first, last = pl.ds(0, 3 * cap), pl.ds(3 * cap, cap)
+
+    def part(s):
+        return pl.ds((0, 1, 3, 2)[s] * cap, cap)
 
     barrier = pltpu.get_barrier_semaphore()
     peers = [pdev(1), pdev(2), pdev(3), qdev(0, 1 - c, c)]
@@ -109,8 +113,8 @@
     def code_rows(s):
         return code if s == 0 else codes.at[s - 1]
 
-    def slots(o):
-        return lax.broadcasted_iota(jnp.int32, (2 * cap, tokens), 0) + qdev(o, 0, c) * cap
+    def slots(o, n=tokens):
+        return lax.broadcasted_iota(jnp.int32, (2 * cap, n), 0) + qdev(o, 0, c) * cap
 
     def pack(s):
         cref = code_rows(s)
@@ -123,7 +127,7 @@
         def one(t, carry):
             cols = pl.ds(pl.multiple_of(t * tile, tile), tile)
             r = jnp.dot(pbuf[...], gref[:, cols], preferred_element_type=f32).astype(bf16)
-            dst = pl.ds(s * cap, cap)
+            dst = part(s)
             for i in range(6):
                 outq[i, dst, cols] = r[i * cap:(i + 1) * cap]
             r0, r1 = r[6 * cap:7 * cap], r[7 * cap:8 * cap]
@@ -149,15 +153,14 @@
     w = w - wa.astype(f32)
     wb = w.astype(bf16)
     wc = (w - wb.astype(f32)).astype(bf16)
-    logits = jnp.dot(hid[...], wc, preferred_element_type=f32) + jnp.dot(hid[...], wb, preferred_element_type=f32)
-    logits = logits + jnp.dot(hid[...], wa, preferred_element_type=f32)
-    ex = jnp.exp(logits - jnp.max(logits, axis=1, keepdims=True))
-    prob = ex / jnp.sum(ex, axis=1, keepdims=True)
-    ecol = lax.broadcasted_iota(jnp.int32, (tokens, experts), 1)
-    p0 = jnp.sum(jnp.where(ids[:, 0:1] == ecol, prob, 0.0), axis=1, keepdims=True)
-    p1 = jnp.sum(jnp.where(ids[:, 1:2] == ecol, prob, 0.0), axis=1, keepdims=True)
-    gate[0] = jnp.broadcast_to(p0 / (p0 + p1), gate.shape[1:])
-    gate[1] = jnp.broadcast_to(p1 / (p0 + p1), gate.shape[1:])
+    terms = lax.dot_general(jnp.concatenate([wc, wb, wa], axis=0), hid[...], (((1,), (1,)), ((), ())), preferred_element_type=f32)
+    logits = (terms[0:experts] + terms[experts:2 * experts]) + terms[2 * experts:]
+    ex = jnp.exp(logits - jnp.max(logits, axis=0, keepdims=True))
+    prob = ex / jnp.sum(ex, axis=0, keepdims=True)
+    p0 = jnp.sum(jnp.where(hot0, prob, 0.0), axis=0, keepdims=True)
+    p1 = jnp.sum(jnp.where(hot1, prob, 0.0), axis=0, keepdims=True)
+    gate[0] = jnp.broadcast_to(p0 / (p0 + p1), (128, tokens)).T
+    gate[1] = jnp.broadcast_to(p1 / (p0 + p1), (128, tokens)).T
 
     got_it(codes.at[0], CODE + 0)
     got_it(got.at[0, hi], GATHER + 1)
@@ -165,21 +168,25 @@
     got_it(codes.at[2], CODE + 2)
     got_it(got.at[2, lo], GATHER + 3)
     pack(3)
+    put(outq.at[0, first], fwd.at[0, first], LEG + 0, LEG + 0, qdev(1, c, c))
+    put(outq.at[1, first], fwd.at[1, first], LEG + 1, LEG + 1, qdev(3, c, c))
     got_it(codes.at[1], CODE + 1)
     got_it(got.at[1, lo], GATHER + 4)
     got_it(got.at[1, hi], GATHER + 5)
     pack(2)
 
-    put(outq.at[0], fwd.at[0], LEG + 0, LEG + 0, qdev(1, c, c))
-    put(outq.at[1], fwd.at[1], LEG + 1, LEG + 1, qdev(3, c, c))
+    put(outq.at[0, last], fwd.at[0, last], LEG + 2, LEG + 2, qdev(1, c, c))
+    put(outq.at[1, last], fwd.at[1, last], LEG + 3, LEG + 3, qdev(3, c, c))
     put(outq.at[2], xs.at[2 + c], SNBR + 0, CHUNK + 2 + c, qdev(1, 0, c))
     put(outq.at[5], xs.at[2 + c], SNBR + 1, CHUNK + 2 + c, qdev(3, 1, c))
     put(outq.at[6], xs.at[1], CHUNK + 1, CHUNK + 1, qdev(0, 1 - c, c))
 
     def chunk_forward():
-        got_it(fwd.at[0], LEG + 0)
+        got_it(fwd.at[0, first], LEG + 0)
+        got_it(fwd.at[0, last], LEG + 2)
         put(fwd.at[0], xs.at[4 + c], SFWD + 0, CHUNK + 4 + c, qdev(1, 0, c))
-        got_it(fwd.at[1], LEG + 1)
+        got_it(fwd.at[1, first], LEG + 1)
+        got_it(fwd.at[1, last], LEG + 3)
         put(fwd.at[1], xs.at[4 + c], SFWD + 1, CHUNK + 4 + c, qdev(3, 1, c))
         put(outq.at[3], xs.at[6 + c], SNBR + 2, CHUNK + 6 + c, qdev(1, 1, c))
         put(outq.at[4], xs.at[6 + c], SNBR + 3, CHUNK + 6 + c, qdev(3, 0, c))
@@ -227,7 +234,7 @@
         lax.fori_loop(0, ffn // ftile, up, 0)
         lax.fori_loop(0, width // tile, down, 0)
 
-    for step in range(8):
+    for step in (0, 1, 2, 3, 5, 4, 6, 7):
         if step:
             got_it(xs.at[step], CHUNK + step)
         expert(step)
@@ -236,15 +243,15 @@
 
     drain()
 
-    def place(s, k, dst):
-        ck = code_rows(s)[k:k + 1, :]
+    def place(s, k, dst, i=0, n=tokens):
+        ck = code_rows(s)[k:k + 1, i * n:(i + 1) * n]
         for o in range(SIDE):
-            pbuf[o * 2 * cap:(o + 1) * 2 * cap, :] = jnp.where(slots(o) == ck, 1.0, 0.0).astype(bf16)
+            pbuf[o * 2 * cap:(o + 1) * 2 * cap, 0:n] = jnp.where(slots(o, n) == ck, 1.0, 0.0).astype(bf16)
 
         def one(t, carry):
             cols = pl.ds(pl.multiple_of(t * tile, tile), tile)
-            rows = back[:, pl.ds(s * cap, cap), cols].reshape(8 * cap, tile)
-            dst[:, cols] = lax.dot_general(pbuf[...], rows, (((0,), (0,)), ((), ())), preferred_element_type=f32).astype(bf16)
+            rows = back[:, part(s), cols].reshape(8 * cap, tile)
+            dst[i * n:(i + 1) * n, cols] = lax.dot_general(pbuf[:, 0:n], rows, (((0,), (0,)), ((), ())), preferred_element_type=f32).astype(bf16)
             return carry
 
         lax.fori_loop(0, width // tile, one, 0)
@@ -252,11 +259,10 @@
     got_it(back.at[1 - c], BACK + 1 - c)
     for blk in (2, 7, 3, 6, 4, 5):
         got_it(back.at[blk], BACK + blk)
-    place(2, 0, outq.at[0])
     for i, h in enumerate((lo, hi)):
+        place(2, 0, outq.at[0], i, half)
         put(outq.at[0, h], lbuf.at[0, h], HOPP + i, HOPP + i, pdev(1))
-    place(2, 1, outq.at[1])
-    for i, h in enumerate((lo, hi)):
+        place(2, 1, outq.at[1], i, half)
         put(outq.at[1, h], lbuf.at[1, h], HOPP + 2 + i, HOPP + 2 + i, pdev(3))
     place(3, 1, outq.at[2])
     put(outq.at[2], rbuf.at[1], HOME + 0, HOME + 0, pdev(1))
@@ -299,7 +305,7 @@
         cp.wait()
 
 
-def fused(hidden, rw, ids, idst, scale, w1, w3, w2, cap):
+def fused(hidden, rw, idst, scale, w1, w3, w2, cap):
     tokens, width = hidden.shape
     ffn = w1.shape[1]
     rows = SIDE * cap
@@ -313,15 +319,15 @@
             jax.ShapeDtypeStruct((2, rows, width), bf),
             jax.ShapeDtypeStruct((2, rows, width), bf),
         ],
-        in_specs=[vm, vm, pl.BlockSpec(memory_space=pltpu.SMEM), hbm, hbm, hbm, hbm, hbm],
+        in_specs=[vm, pl.BlockSpec(memory_space=pltpu.SMEM), hbm, hbm, hbm, hbm, hbm],
         out_specs=[hbm, hbm, hbm],
         scratch_shapes=[
             pltpu.VMEM((tokens, width), bf),
             pltpu.VMEM(rw.shape, jnp.float32),
             pltpu.VMEM((width, ffn), bf), pltpu.VMEM((width, ffn), bf), pltpu.VMEM((ffn, width), bf),
             pltpu.VMEM((3, tokens, width), bf),
-            pltpu.VMEM(idst.shape, jnp.int32),
-            pltpu.VMEM((3,) + idst.shape, jnp.int32),
+            pltpu.VMEM((8, tokens), jnp.int32),
+            pltpu.VMEM((3, 8, tokens), jnp.int32),
             pltpu.VMEM((2, tokens, 128), jnp.float32),
             pltpu.VMEM((8 * cap, tokens), bf),
             pltpu.VMEM((8, rows, width), bf),
@@ -336,7 +342,7 @@
         ],
         compiler_params=pltpu.CompilerParams(has_side_effects=True, collective_id=0, vmem_limit_bytes=67043328),
         name='moe',
-    )(ids, idst, scale, hidden, rw, w1, w3, w2)[0]
+    )(idst, scale, hidden, rw, w1, w3, w2)[0]
 
 
 def solution(mesh):
@@ -346,8 +352,7 @@
         tokens = hidden.shape[0]
         experts = w_gate.shape[0] * ep_size
         cap = tokens // max(1, experts // 8)
-        idst = jnp.pad(expert_ids.T, ((0, 6), (0, 0)))
-        return fused(hidden, router_w, expert_ids, idst, post_scale, w_gate[0], w_up[0], w_down[0], cap)
+        return fused(hidden, router_w.T, expert_ids.T, post_scale, w_gate[0], w_up[0], w_down[0], cap)
 
     tok_spec = P(('dp', 'ep'))
     return jax.shard_map(local_step, mesh=mesh, in_specs=(tok_spec, P(), tok_spec, P('ep'), P('ep'), P('ep'), P()), out_specs=tok_spec, check_vma=False)

time: 172 us -> 161 us (0.936)
  Pallas kernels: 165 us -> 159 us
  local copies, waits for them, and re-layouts: 7.31 us -> 2.3 us
    pallas_call x1, Pallas kernels: 165 us -> 159 us  [fused(): pl.pallas_call(kernel_body, out_shape=[jax.ShapeDtypeStruct((tokens, widt...]
    unnamed x3 -> x1, local copies, waits for them, and re-layouts: 6.03 us -> 2.3 us
where the time goes in v3:
time: 161 us
  Pallas kernels  159 us (99%)
  local copies, waits for them, and re-layouts  2.3 us (1%)
    pallas_call x1, Pallas kernels, fused(): pl.pallas_call(kernel_body, out_shape=[jax.ShapeDtypeStruct((tokens, widt...  159 us

profile of v3, /device:TPU:97, one launch (start us, length us, event | category | flops | bytes accessed | tf_op | source)
XLA Modules:
  0.0 161.2 jit_solution(7448999603102082440)
XLA Ops:
  0.0 158.9 %moe.1 = (bf16[256,2048]{1,0:T(8,128)(2,1)}, bf16[2,256,2048]{2,1,0:T(8,128)(2,1)}, bf16[2,256,2048]{2,1,0:T(8,128)(2,1)}) custom-call(s32[2,256]{1,0:T(2,128)} %bitcast.9, f32[2]{0:T(128)} %scale.1, bf16[256,2048]{1,0:T(8,128)(2,1)} %hidh.1, f32[32,2048]{1,0:T(8,128)} %bitcast.8, bf16[2048,2048]{1,0:T(8,128)(2,1)} %bitcast.5, bf16[2048,2048]{1,0:T(8,128)(2,1)} %bitcast.6, ...), custom_call_target="tpu_custom_call" | custom-call | tf_op jit(solution)/shard_map/moe/pallas_call | solution.py:315
  158.9 2.3 %copy.9 = bf16[256,2048]{1,0:T(8,128)(2,1)} copy(bf16[256,2048]{1,0:T(8,128)(2,1)} %get-tuple-element.6) | data formatting | bytes 2097152

commit v4 on v3

--- a/solution.py
+++ b/solution.py
@@ -14,15 +14,15 @@
 CHUNK = 9
 LEG = 17
 BACK = 21
-BLEG = 29
-HOPP = 31
-HOME = 35
-NMSG = 41
-SFWD = 41
-SBFWD = 43
-SNBR = 45
-SBACK = 49
-NSEND = 56
+BLEG = 37
+HOPP = 41
+HOME = 45
+NMSG = 53
+SFWD = 53
+SBFWD = 55
+SNBR = 59
+SBACK = 63
+NSEND = 77
 LHID, LRW, LW1, LW3, LW2, LOUT = 0, 1, 2, 3, 4, 5
 
 
@@ -35,7 +35,9 @@
     ffn = w1.shape[1]
     experts = rw.shape[0]
     half = tokens // 2
-    tile = min(512, width)
+    tile = min(512, width // 2)
+    wide = width // 2
+    sides = (pl.ds(0, wide), pl.ds(wide, wide))
     ftile = min(512, ffn)
     f32, bf16 = jnp.float32, jnp.bfloat16
     me = lax.axis_index('ep')
@@ -60,8 +62,8 @@
         cp.start()
         sent.append((src, sid))
 
-    def drain():
-        while sent:
+    def drain(n=None):
+        for _ in range(len(sent) if n is None else n):
             src, sid = sent.pop(0)
             rcopy(src, src, sid, 0, me).wait_send()
 
@@ -191,25 +193,21 @@
         put(outq.at[3], xs.at[6 + c], SNBR + 2, CHUNK + 6 + c, qdev(1, 1, c))
         put(outq.at[4], xs.at[6 + c], SNBR + 3, CHUNK + 6 + c, qdev(3, 0, c))
 
-    def back_forward():
-        got_it(bleg.at[0], BLEG + 0)
-        put(bleg.at[0], back.at[4], SBFWD + 0, BACK + 4, qdev(1, c, c))
-        got_it(bleg.at[1], BLEG + 1)
-        put(bleg.at[1], back.at[5], SBFWD + 1, BACK + 5, qdev(3, c, c))
-
-    def after(step):
-        k = step % 2
+    def back_forward(f):
+        for i, o in enumerate((1, 3)):
+            got_it(bleg.at[i, :, sides[f]], BLEG + 2 * f + i)
+            put(bleg.at[i, :, sides[f]], back.at[4 + i, :, sides[f]], SBFWD + 2 * f + i, BACK + 8 * f + 4 + i, qdev(o, c, c))
+
+    def after(step, f):
+        k, sid = step % 2, SBACK + 2 * (step - 1)
         if step == 1:
-            put(xs.at[1], back.at[c], SBACK + 0, BACK + c, qdev(0, 1 - c, c))
-            chunk_forward()
+            put(xs.at[1], back.at[c], sid, BACK + c, qdev(0, 1 - c, c))
         elif step in (2, 3):
-            put(xs.at[step], back.at[2 + 5 * c], SBACK + step - 1, BACK + 2 + 5 * c, qdev(3 + 2 * c, k, k))
+            put(xs.at[step], back.at[2 + 5 * c], sid, BACK + 2 + 5 * c, qdev(3 + 2 * c, k, k))
         elif step in (4, 5):
-            put(xs.at[step], bleg.at[c], SBACK + step - 1, BLEG + c, qdev(1 + 2 * c, k, k))
+            put(xs.at[step, :, sides[f]], bleg.at[c, :, sides[f]], sid + f, BLEG + 2 * f + c, qdev(1 + 2 * c, k, k))
         else:
-            put(xs.at[step], back.at[6 - 3 * c], SBACK + step - 1, BACK + 6 - 3 * c, qdev(1 + 2 * c, k, k))
-            if step == 6:
-                back_forward()
+            put(xs.at[step, :, sides[f]], back.at[6 - 3 * c, :, sides[f]], sid + f, BACK + 8 * f + 6 - 3 * c, qdev(1 + 2 * c, k, k))
 
     for cp in loads:
         cp.wait()
@@ -232,74 +230,101 @@
             return carry
 
         lax.fori_loop(0, ffn // ftile, up, 0)
-        lax.fori_loop(0, width // tile, down, 0)
-
-    for step in (0, 1, 2, 3, 5, 4, 6, 7):
+        if step == 7:
+            back_forward(1)
+        tiles = width // tile
+        if step < 4:
+            lax.fori_loop(0, tiles, down, 0)
+            if step:
+                after(step, 0)
+        else:
+            lax.fori_loop(0, tiles // 2, down, 0)
+            after(step, 0)
+            lax.fori_loop(tiles // 2, tiles, down, 0)
+            after(step, 1)
+
+    for step in range(8):
         if step:
             got_it(xs.at[step], CHUNK + step)
         expert(step)
-        if step:
-            after(step)
-
-    drain()
-
-    def place(s, k, dst, i=0, n=tokens):
-        ck = code_rows(s)[k:k + 1, i * n:(i + 1) * n]
+        if step == 1:
+            chunk_forward()
+            chunks_sent = len(sent)
+        elif step == 6:
+            back_forward(0)
+
+    drain(chunks_sent)
+
+    def place(s, k, dst, f):
+        ck = code_rows(s)[k:k + 1, :]
         for o in range(SIDE):
-            pbuf[o * 2 * cap:(o + 1) * 2 * cap, 0:n] = jnp.where(slots(o, n) == ck, 1.0, 0.0).astype(bf16)
+            pbuf[o * 2 * cap:(o + 1) * 2 * cap, :] = jnp.where(slots(o) == ck, 1.0, 0.0).astype(bf16)
 
         def one(t, carry):
-            cols = pl.ds(pl.multiple_of(t * tile, tile), tile)
+            cols = pl.ds(pl.multiple_of(f * wide + t * tile, tile), tile)
             rows = back[:, part(s), cols].reshape(8 * cap, tile)
-            dst[i * n:(i + 1) * n, cols] = lax.dot_general(pbuf[:, 0:n], rows, (((0,), (0,)), ((), ())), preferred_element_type=f32).astype(bf16)
-            return carry
-
-        lax.fori_loop(0, width // tile, one, 0)
+            dst[:, cols] = lax.dot_general(pbuf[...], rows, (((0,), (0,)), ((), ())), preferred_element_type=f32).astype(bf16)
+            return carry
+
+        lax.fori_loop(0, wide // tile, one, 0)
+
+    def unmerged(f):
+        h = sides[f]
+        for i, (k, o) in enumerate(((0, 1), (1, 3))):
+            place(2, k, outq.at[i], f)
+            put(outq.at[i, :, h], lbuf.at[i, :, h], HOPP + 2 * f + i, HOPP + 2 * f + i, pdev(o))
+        for i, (s, k, o) in enumerate(((3, 1, 1), (1, 0, 3))):
+            place(s, k, outq.at[2 + i], f)
+            put(outq.at[2 + i, :, h], rbuf.at[1 + i, :, h], HOME + 2 * f + i, HOME + 2 * f + i, pdev(o))
+
+    def mergeable(f):
+        place(3, 0, outq.at[4], f)
+        place(1, 1, outq.at[5], f)
+
+    def merged(f):
+        h = sides[f]
+        for i, o in enumerate((1, 3)):
+            got_it(lbuf.at[i, :, h], HOPP + 2 * f + i)
+            outq[4 + i, :, h] = outq[4 + i, :, h] + lbuf[i, :, h]
+            put(outq.at[4 + i, :, h], rbuf.at[3 * i, :, h], HOME + 4 + 2 * f + i, HOME + 4 + 2 * f + i, pdev(o))
 
     got_it(back.at[1 - c], BACK + 1 - c)
-    for blk in (2, 7, 3, 6, 4, 5):
+    for blk in (2, 7):
         got_it(back.at[blk], BACK + blk)
-    for i, h in enumerate((lo, hi)):
-        place(2, 0, outq.at[0], i, half)
-        put(outq.at[0, h], lbuf.at[0, h], HOPP + i, HOPP + i, pdev(1))
-        place(2, 1, outq.at[1], i, half)
-        put(outq.at[1, h], lbuf.at[1, h], HOPP + 2 + i, HOPP + 2 + i, pdev(3))
-    place(3, 1, outq.at[2])
-    put(outq.at[2], rbuf.at[1], HOME + 0, HOME + 0, pdev(1))
-    place(1, 0, outq.at[3])
-    put(outq.at[3], rbuf.at[2], HOME + 1, HOME + 1, pdev(3))
-    place(3, 0, outq.at[4])
-    place(1, 1, outq.at[5])
-    for i, h in enumerate((lo, hi)):
-        got_it(lbuf.at[0, h], HOPP + i)
-        outq[4, h, :] = outq[4, h, :] + lbuf[0, h, :]
-        put(outq.at[4, h], rbuf.at[0, h], HOME + 2 + i, HOME + 2 + i, pdev(1))
-        got_it(lbuf.at[1, h], HOPP + 2 + i)
-        outq[5, h, :] = outq[5, h, :] + lbuf[1, h, :]
-        put(outq.at[5, h], rbuf.at[3, h], HOME + 4 + i, HOME + 4 + i, pdev(3))
-    place(0, 0, got.at[0])
-    place(0, 1, got.at[1])
-    got_it(rbuf.at[1], HOME + 0)
-    got_it(rbuf.at[2], HOME + 1)
-    step_rows = min(64, half)
+    for f in range(2):
+        for blk in (3, 6, 4, 5):
+            got_it(back.at[blk, :, sides[f]], BACK + 8 * f + blk)
+        unmerged(f)
+        if f == 0:
+            mergeable(0)
+    merged(0)
+    mergeable(1)
+    merged(1)
+    for k in range(2):
+        for f in range(2):
+            place(0, k, got.at[k], f)
+    step_rows = min(64, tokens)
     outs = []
-    for i, h in enumerate((lo, hi)):
-        got_it(rbuf.at[0, h], HOME + 2 + i)
-        got_it(rbuf.at[3, h], HOME + 4 + i)
+    for f in range(2):
+        h = sides[f]
+        for i in range(2):
+            got_it(rbuf.at[1 + i, :, h], HOME + 2 * f + i)
+        for i in range(2):
+            got_it(rbuf.at[3 * i, :, h], HOME + 4 + 2 * f + i)
 
         def finish(j, carry):
-            r = pl.ds(pl.multiple_of(i * half + j * step_rows, step_rows), step_rows)
+            r = pl.ds(pl.multiple_of(j * step_rows, step_rows), step_rows)
             g0, g1 = gate[0, r, 0:1], gate[1, r, 0:1]
-            for t in range(width // tile):
-                cols = pl.ds(t * tile, tile)
+            for t in range(wide // tile):
+                cols = pl.ds(f * wide + t * tile, tile)
                 y0 = (got[0, r, cols] + rbuf[0, r, cols] + rbuf[2, r, cols]).astype(f32)
                 y1 = (got[1, r, cols] + rbuf[1, r, cols] + rbuf[3, r, cols]).astype(f32)
                 mixed = g0 * y0 + g1 * y1
                 outq[6, r, cols] = (scale[0] * hid[r, cols].astype(f32) + scale[1] * mixed).astype(bf16)
             return carry
 
-        lax.fori_loop(0, half // step_rows, finish, 0)
-        outs.append(fetch(outq.at[6, h], out.at[h], LOUT + i))
+        lax.fori_loop(0, tokens // step_rows, finish, 0)
+        outs.append(fetch(outq.at[6, :, h], out.at[:, h], LOUT + f))
     drain()
     for cp in outs:
         cp.wait()

time: 161 us -> 157 us (0.975)
  Pallas kernels: 159 us -> 155 us
    pallas_call x1, Pallas kernels: 159 us -> 155 us  [fused(): pl.pallas_call(kernel_body, out_shape=[jax.ShapeDtypeStruct((tokens, widt...]
where the time goes in v4:
time: 157 us
  Pallas kernels  155 us (99%)
  local copies, waits for them, and re-layouts  2.3 us (1%)
    pallas_call x1, Pallas kernels, fused(): pl.pallas_call(kernel_body, out_shape=[jax.ShapeDtypeStruct((tokens, widt...  155 us

profile of v4, /device:TPU:97, one launch (start us, length us, event | category | flops | bytes accessed | tf_op | source)
XLA Modules:
  0.0 156.8 jit_solution(10527091457516935252)
XLA Ops:
  0.0 154.5 %moe.1 = (bf16[256,2048]{1,0:T(8,128)(2,1)}, bf16[2,256,2048]{2,1,0:T(8,128)(2,1)}, bf16[2,256,2048]{2,1,0:T(8,128)(2,1)}) custom-call(s32[2,256]{1,0:T(2,128)} %bitcast.9, f32[2]{0:T(128)} %scale.1, bf16[256,2048]{1,0:T(8,128)(2,1)} %hidh.1, f32[32,2048]{1,0:T(8,128)} %bitcast.8, bf16[2048,2048]{1,0:T(8,128)(2,1)} %bitcast.5, bf16[2048,2048]{1,0:T(8,128)(2,1)} %bitcast.6, ...), custom_call_target="tpu_custom_call" | custom-call | tf_op jit(solution)/shard_map/moe/pallas_call | solution.py:340
  154.5 2.3 %copy.9 = bf16[256,2048]{1,0:T(8,128)(2,1)} copy(bf16[256,2048]{1,0:T(8,128)(2,1)} %get-tuple-element.6) | data formatting | bytes 2097152

commit v5 on v4

--- a/solution.py
+++ b/solution.py
@@ -23,12 +23,12 @@
 SNBR = 59
 SBACK = 63
 NSEND = 77
-LHID, LRW, LW1, LW3, LW2, LOUT = 0, 1, 2, 3, 4, 5
-
-
-def kernel_body(idst, scale, hidh, rwh, w1h, w3h, w2h,
+LHID, LRW, LW1, LW3, LW2, LOUT, LIDS = 0, 1, 2, 3, 4, 5, 7
+
+
+def kernel_body(idsh, scale, hidh, rwh, w1h, w3h, w2h,
                 out, fwd, bleg,
-                hid, rw, w1, w3, w2, got, code, codes, gate, pbuf, xs, outq, mid, back, lbuf, rbuf,
+                idst, hid, rw, w1, w3, w2, got, code, codes, gate, pbuf, xs, outq, mid, back, lbuf, rbuf,
                 send, recv, lsem):
     tokens, width = hid.shape
     cap = xs.shape[1] // SIDE
@@ -88,14 +88,18 @@
     for to in peers:
         pl.semaphore_signal(barrier, inc=1, device_id={'ep': to}, device_id_type=MESH)
     load_hid = fetch(hidh, hid, LHID)
+    load_ids = fetch(idsh, idst, LIDS)
+    pl.semaphore_wait(barrier, len(peers))
+
+    load_hid.wait()
+    put(hid.at[lo], got.at[0, lo], GATHER + 0, GATHER + 0, pdev(1))
+    put(hid.at[hi], got.at[2, hi], GATHER + 2, GATHER + 2, pdev(3))
+    put(hid.at[hi], got.at[0, hi], GATHER + 1, GATHER + 1, pdev(1))
+    put(hid.at[lo], got.at[2, lo], GATHER + 3, GATHER + 3, pdev(3))
     load_rw = fetch(rwh, rw, LRW)
-    pl.semaphore_wait(barrier, len(peers))
-
-    put(hidh.at[lo], got.at[0, lo], GATHER + 0, GATHER + 0, pdev(1))
-    put(hidh.at[hi], got.at[2, hi], GATHER + 2, GATHER + 2, pdev(3))
-    put(hidh.at[hi], got.at[0, hi], GATHER + 1, GATHER + 1, pdev(1))
-    put(hidh.at[lo], got.at[2, lo], GATHER + 3, GATHER + 3, pdev(3))
     loads = [fetch(w1h, w1, LW1), fetch(w3h, w3, LW3), fetch(w2h, w2, LW2)]
+
+    load_ids.wait()
 
     erow = lax.broadcasted_iota(jnp.int32, (experts, tokens), 0)
     hot0, hot1 = idst[0:1, :] == erow, idst[1:2, :] == erow
@@ -140,7 +144,6 @@
 
         lax.fori_loop(0, width // tile, one, 0)
 
-    load_hid.wait()
     pack(0)
     for s, o in ((1, 1), (3, 3), (2, 2)):
         put(code, codes.at[s - 1], CODE + s - 1, CODE + s - 1, pdev(o))
@@ -335,7 +338,6 @@
     ffn = w1.shape[1]
     rows = SIDE * cap
     bf = jnp.bfloat16
-    vm = pl.BlockSpec(memory_space=pltpu.VMEM)
     hbm = pl.BlockSpec(memory_space=pl.ANY)
     return pl.pallas_call(
         kernel_body,
@@ -344,9 +346,10 @@
             jax.ShapeDtypeStruct((2, rows, width), bf),
             jax.ShapeDtypeStruct((2, rows, width), bf),
         ],
-        in_specs=[vm, pl.BlockSpec(memory_space=pltpu.SMEM), hbm, hbm, hbm, hbm, hbm],
+        in_specs=[hbm, pl.BlockSpec(memory_space=pltpu.SMEM), hbm, hbm, hbm, hbm, hbm],
         out_specs=[hbm, hbm, hbm],
         scratch_shapes=[
+            pltpu.VMEM(idst.shape, jnp.int32),
             pltpu.VMEM((tokens, width), bf),
             pltpu.VMEM(rw.shape, jnp.float32),
             pltpu.VMEM((width, ffn), bf), pltpu.VMEM((width, ffn), bf), pltpu.VMEM((ffn, width), bf),
@@ -363,7 +366,7 @@
             pltpu.VMEM((4, tokens, width), bf),
             pltpu.SemaphoreType.DMA((NSEND,)),
             pltpu.SemaphoreType.DMA((NMSG,)),
-            pltpu.SemaphoreType.DMA((7,)),
+            pltpu.SemaphoreType.DMA((8,)),
         ],
         compiler_params=pltpu.CompilerParams(has_side_effects=True, collective_id=0, vmem_limit_bytes=67043328),
         name='moe',
@@ -377,7 +380,8 @@
         tokens = hidden.shape[0]
         experts = w_gate.shape[0] * ep_size
         cap = tokens // max(1, experts // 8)
-        return fused(hidden, router_w.T, expert_ids.T, post_scale, w_gate[0], w_up[0], w_down[0], cap)
+        out = fused(hidden, router_w.T, expert_ids.T, post_scale, w_gate[0], w_up[0], w_down[0], cap)
+        return jnp.where(jnp.isnan(out), jnp.nan, out)
 
     tok_spec = P(('dp', 'ep'))
     return jax.shard_map(local_step, mesh=mesh, in_specs=(tok_spec, P(), tok_spec, P('ep'), P('ep'), P('ep'), P()), out_specs=tok_spec, check_vma=False)

time: 157 us -> 157 us (level)
  local copies, waits for them, and re-layouts: 2.3 us -> 0 us
  other arithmetic: 0 us -> 2.29 us
    unnamed x1 -> x0, local copies, waits for them, and re-layouts: 2.3 us -> none
    select_n x0 -> x1, other arithmetic: none -> 2.29 us  [local_step(): return jnp.where(jnp.isnan(out), jnp.nan, out)]
where the time goes in v5:
time: 157 us
  Pallas kernels  154 us (98%)
  other arithmetic  2.29 us (1%)
    pallas_call x1, Pallas kernels, fused(): pl.pallas_call(kernel_body, out_shape=[jax.ShapeDtypeStruct((tokens, widt...  154 us

profile of v5, /device:TPU:97, one launch (start us, length us, event | category | flops | bytes accessed | tf_op | source)
XLA Modules:
  0.0 156.7 jit_solution(7305280902895135006)
XLA Ops:
  0.0 154.4 %moe.1 = (bf16[256,2048]{1,0:T(8,128)(2,1)}, bf16[2,256,2048]{2,1,0:T(8,128)(2,1)}, bf16[2,256,2048]{2,1,0:T(8,128)(2,1)}) custom-call(s32[2,256]{1,0:T(2,128)} %bitcast.9, f32[2]{0:T(128)} %scale.1, bf16[256,2048]{1,0:T(8,128)(2,1)} %hidh.1, f32[32,2048]{1,0:T(8,128)} %bitcast.8, bf16[2048,2048]{1,0:T(8,128)(2,1)} %bitcast.5, bf16[2048,2048]{1,0:T(8,128)(2,1)} %bitcast.6, ...), custom_call_target="tpu_custom_call" | custom-call | tf_op jit(solution)/shard_map/moe/pallas_call | solution.py:342
  154.4 2.3 %compare_select_fusion = bf16[256,2048]{1,0:T(8,128)(2,1)} fusion(bf16[256,2048]{1,0:T(8,128)(2,1)} %get-tuple-element.6), kind=kLoop, calls=%fused_computation | loop fusion | flops 1048576 | bytes 2097152 | tf_op jit(solution)/shard_map/jit(_where)/select_n | solution.py:384

commit v6 on v5

--- a/solution.py
+++ b/solution.py
@@ -17,12 +17,12 @@
 BLEG = 37
 HOPP = 41
 HOME = 45
-NMSG = 53
-SFWD = 53
-SBFWD = 55
-SNBR = 59
-SBACK = 63
-NSEND = 77
+NMSG = 57
+SFWD = 57
+SBFWD = 59
+SNBR = 63
+SBACK = 67
+NSEND = 81
 LHID, LRW, LW1, LW3, LW2, LOUT, LIDS = 0, 1, 2, 3, 4, 5, 7
 
 
@@ -288,8 +288,10 @@
         h = sides[f]
         for i, o in enumerate((1, 3)):
             got_it(lbuf.at[i, :, h], HOPP + 2 * f + i)
-            outq[4 + i, :, h] = outq[4 + i, :, h] + lbuf[i, :, h]
-            put(outq.at[4 + i, :, h], rbuf.at[3 * i, :, h], HOME + 4 + 2 * f + i, HOME + 4 + 2 * f + i, pdev(o))
+            for j, r in enumerate((lo, hi)):
+                sid = HOME + 4 + 4 * f + 2 * i + j
+                outq[4 + i, r, h] = outq[4 + i, r, h] + lbuf[i, r, h]
+                put(outq.at[4 + i, r, h], rbuf.at[3 * i, r, h], sid, sid, pdev(o))
 
     got_it(back.at[1 - c], BACK + 1 - c)
     for blk in (2, 7):
@@ -306,31 +308,28 @@
     for k in range(2):
         for f in range(2):
             place(0, k, got.at[k], f)
-    step_rows = min(64, tokens)
-    outs = []
+    step_rows = min(64, half)
     for f in range(2):
         h = sides[f]
         for i in range(2):
             got_it(rbuf.at[1 + i, :, h], HOME + 2 * f + i)
-        for i in range(2):
-            got_it(rbuf.at[3 * i, :, h], HOME + 4 + 2 * f + i)
-
-        def finish(j, carry):
-            r = pl.ds(pl.multiple_of(j * step_rows, step_rows), step_rows)
-            g0, g1 = gate[0, r, 0:1], gate[1, r, 0:1]
-            for t in range(wide // tile):
-                cols = pl.ds(f * wide + t * tile, tile)
-                y0 = (got[0, r, cols] + rbuf[0, r, cols] + rbuf[2, r, cols]).astype(f32)
-                y1 = (got[1, r, cols] + rbuf[1, r, cols] + rbuf[3, r, cols]).astype(f32)
-                mixed = g0 * y0 + g1 * y1
-                outq[6, r, cols] = (scale[0] * hid[r, cols].astype(f32) + scale[1] * mixed).astype(bf16)
-            return carry
-
-        lax.fori_loop(0, tokens // step_rows, finish, 0)
-        outs.append(fetch(outq.at[6, :, h], out.at[:, h], LOUT + f))
+        for m, part_rows in enumerate((lo, hi)):
+            for i in range(2):
+                got_it(rbuf.at[3 * i, part_rows, h], HOME + 4 + 4 * f + 2 * i + m)
+
+            def finish(j, carry):
+                r = pl.ds(pl.multiple_of(m * half + j * step_rows, step_rows), step_rows)
+                g0, g1 = gate[0, r, 0:1], gate[1, r, 0:1]
+                for t in range(wide // tile):
+                    cols = pl.ds(f * wide + t * tile, tile)
+                    y0 = (got[0, r, cols] + rbuf[0, r, cols] + rbuf[2, r, cols]).astype(f32)
+                    y1 = (got[1, r, cols] + rbuf[1, r, cols] + rbuf[3, r, cols]).astype(f32)
+                    mixed = g0 * y0 + g1 * y1
+                    out[r, cols] = (scale[0] * hid[r, cols].astype(f32) + scale[1] * mixed).astype(bf16)
+                return carry
+
+            lax.fori_loop(0, half // step_rows, finish, 0)
     drain()
-    for cp in outs:
-        cp.wait()
 
 
 def fused(hidden, rw, idst, scale, w1, w3, w2, cap):
@@ -342,12 +341,12 @@
     return pl.pallas_call(
         kernel_body,
         out_shape=[
-            jax.ShapeDtypeStruct((tokens, width), bf),
+            pltpu.VMEM((tokens, width), bf),
             jax.ShapeDtypeStruct((2, rows, width), bf),
             jax.ShapeDtypeStruct((2, rows, width), bf),
         ],
         in_specs=[hbm, pl.BlockSpec(memory_space=pltpu.SMEM), hbm, hbm, hbm, hbm, hbm],
-        out_specs=[hbm, hbm, hbm],
+        out_specs=[pl.BlockSpec(memory_space=pltpu.VMEM), hbm, hbm],
         scratch_shapes=[
             pltpu.VMEM(idst.shape, jnp.int32),
             pltpu.VMEM((tokens, width), bf),
@@ -368,7 +367,7 @@
             pltpu.SemaphoreType.DMA((NMSG,)),
             pltpu.SemaphoreType.DMA((8,)),
         ],
-        compiler_params=pltpu.CompilerParams(has_side_effects=True, collective_id=0, vmem_limit_bytes=67043328),
+        compiler_params=pltpu.CompilerParams(has_side_effects=True, collective_id=0, vmem_limit_bytes=64000000),
         name='moe',
     )(idst, scale, hidden, rw, w1, w3, w2)[0]
 
@@ -381,7 +380,7 @@
         experts = w_gate.shape[0] * ep_size
         cap = tokens // max(1, experts // 8)
         out = fused(hidden, router_w.T, expert_ids.T, post_scale, w_gate[0], w_up[0], w_down[0], cap)
-        return jnp.where(jnp.isnan(out), jnp.nan, out)
+        return out
 
     tok_spec = P(('dp', 'ep'))
     return jax.shard_map(local_step, mesh=mesh, in_specs=(tok_spec, P(), tok_spec, P('ep'), P('ep'), P('ep'), P()), out_specs=tok_spec, check_vma=False)

time: 157 us -> 155 us (0.987)
  other arithmetic: 2.29 us -> 0 us
    select_n x1 -> x0, other arithmetic: 2.29 us -> none  [local_step(): return jnp.where(jnp.isnan(out), jnp.nan, out)]
where the time goes in v6:
time: 155 us; the launch traced here: 154 us
  Pallas kernels  153 us (99%)
    pallas_call x1, Pallas kernels, fused(): pl.pallas_call(kernel_body, out_shape=[pltpu.VMEM((tokens, width), bf), j...  153 us

profile of v6, /device:TPU:97, one launch (start us, length us, event | category | flops | bytes accessed | tf_op | source)
XLA Modules:
  0.0 154.4 jit_solution(17536860237502964701)
XLA Ops:
  0.0 153.4 %moe.1 = (bf16[256,2048]{1,0:T(8,128)(2,1)S(1)}, bf16[2,256,2048]{2,1,0:T(8,128)(2,1)}, bf16[2,256,2048]{2,1,0:T(8,128)(2,1)}) custom-call(s32[2,256]{1,0:T(2,128)} %bitcast.9, f32[2]{0:T(128)} %scale.1, bf16[256,2048]{1,0:T(8,128)(2,1)} %hidh.1, f32[32,2048]{1,0:T(8,128)} %bitcast.8, bf16[2048,2048]{1,0:T(8,128)(2,1)} %bitcast.5, ...), custom_call_target="tpu_custom_call" | custom-call | tf_op jit(solution)/shard_map/moe/pallas_call | solution.py:341
  153.4 1.0 copy.9

commit v7 on v6

--- a/solution.py
+++ b/solution.py
@@ -27,8 +27,8 @@
 
 
 def kernel_body(idsh, scale, hidh, rwh, w1h, w3h, w2h,
-                out, fwd, bleg,
-                idst, hid, rw, w1, w3, w2, got, code, codes, gate, pbuf, xs, outq, mid, back, lbuf, rbuf,
+                out, fwd,
+                idst, hid, rw, w1, w3, w2, got, code, codes, gate, pbuf, xs, outq, mid, back, bleg, lbuf, rbuf,
                 send, recv, lsem):
     tokens, width = hid.shape
     cap = xs.shape[1] // SIDE
@@ -343,10 +343,9 @@
         out_shape=[
             pltpu.VMEM((tokens, width), bf),
             jax.ShapeDtypeStruct((2, rows, width), bf),
-            jax.ShapeDtypeStruct((2, rows, width), bf),
         ],
         in_specs=[hbm, pl.BlockSpec(memory_space=pltpu.SMEM), hbm, hbm, hbm, hbm, hbm],
-        out_specs=[pl.BlockSpec(memory_space=pltpu.VMEM), hbm, hbm],
+        out_specs=[pl.BlockSpec(memory_space=pltpu.VMEM), hbm],
         scratch_shapes=[
             pltpu.VMEM(idst.shape, jnp.int32),
             pltpu.VMEM((tokens, width), bf),
@@ -361,13 +360,14 @@
             pltpu.VMEM((7, rows, width), bf),
             pltpu.VMEM((rows, ffn), bf),
             pltpu.VMEM((8, rows, width), bf),
+            pltpu.VMEM((2, rows, width), bf),
             pltpu.VMEM((2, tokens, width), bf),
             pltpu.VMEM((4, tokens, width), bf),
             pltpu.SemaphoreType.DMA((NSEND,)),
             pltpu.SemaphoreType.DMA((NMSG,)),
             pltpu.SemaphoreType.DMA((8,)),
         ],
-        compiler_params=pltpu.CompilerParams(has_side_effects=True, collective_id=0, vmem_limit_bytes=64000000),
+        compiler_params=pltpu.CompilerParams(has_side_effects=True, collective_id=0, vmem_limit_bytes=65800000),
         name='moe',
     )(idst, scale, hidden, rw, w1, w3, w2)[0]
 

time: 155 us -> 155 us (level)
  no operation moved by 1% of the time
where the time goes in v7:
time: 155 us; the launch traced here: 154 us
  Pallas kernels  153 us (99%)
    pallas_call x1, Pallas kernels, fused(): pl.pallas_call(kernel_body, out_shape=[pltpu.VMEM((tokens, width), bf), j...  153 us

profile of v7, /device:TPU:97, one launch (start us, length us, event | category | flops | bytes accessed | tf_op | source)
XLA Modules:
  0.0 154.4 jit_solution(8308374084692167667)
XLA Ops:
  0.0 153.4 %moe.1 = (bf16[256,2048]{1,0:T(8,128)(2,1)S(1)}, bf16[2,256,2048]{2,1,0:T(8,128)(2,1)}) custom-call(s32[2,256]{1,0:T(2,128)} %bitcast.9, f32[2]{0:T(128)} %scale.1, bf16[256,2048]{1,0:T(8,128)(2,1)} %hidh.1, f32[32,2048]{1,0:T(8,128)} %bitcast.8, bf16[2048,2048]{1,0:T(8,128)(2,1)} %bitcast.5, bf16[2048,2048]{1,0:T(8,128)(2,1)} %bitcast.6, ...), custom_call_target="tpu_custom_call" | custom-call | tf_op jit(solution)/shard_map/moe/pallas_call | solution.py:341
  153.4 1.0 copy.9

commit v8 on v6

--- a/solution.py
+++ b/solution.py
@@ -38,7 +38,8 @@
     tile = min(512, width // 2)
     wide = width // 2
     sides = (pl.ds(0, wide), pl.ds(wide, wide))
-    ftile = min(512, ffn)
+    dtile = min(1024, wide)
+    ftile = min(1024, ffn)
     f32, bf16 = jnp.float32, jnp.bfloat16
     me = lax.axis_index('ep')
     y, x, c = lax.div(me, 2 * SIDE), lax.rem(lax.div(me, 2), SIDE), lax.rem(me, 2)
@@ -224,7 +225,7 @@
             return carry
 
         def down(t, carry):
-            cols = pl.ds(pl.multiple_of(t * tile, tile), tile)
+            cols = pl.ds(pl.multiple_of(t * dtile, dtile), dtile)
             r = jnp.dot(mid[...], w2[:, cols], preferred_element_type=f32).astype(bf16)
             if step == 0:
                 back[c, :, cols] = r
@@ -235,7 +236,7 @@
         lax.fori_loop(0, ffn // ftile, up, 0)
         if step == 7:
             back_forward(1)
-        tiles = width // tile
+        tiles = width // dtile
         if step < 4:
             lax.fori_loop(0, tiles, down, 0)
             if step:
@@ -367,7 +368,7 @@
             pltpu.SemaphoreType.DMA((NMSG,)),
             pltpu.SemaphoreType.DMA((8,)),
         ],
-        compiler_params=pltpu.CompilerParams(has_side_effects=True, collective_id=0, vmem_limit_bytes=64000000),
+        compiler_params=pltpu.CompilerParams(has_side_effects=True, collective_id=0, vmem_limit_bytes=65500000),
         name='moe',
     )(idst, scale, hidden, rw, w1, w3, w2)[0]
 

time: 155 us -> 154 us (level)
  no operation moved by 1% of the time
where the time goes in v8:
time: 154 us
  Pallas kernels  153 us (99%)
    pallas_call x1, Pallas kernels, fused(): pl.pallas_call(kernel_body, out_shape=[pltpu.VMEM((tokens, width), bf), j...  153 us

profile of v8, /device:TPU:97, one launch (start us, length us, event | category | flops | bytes accessed | tf_op | source)
XLA Modules:
  0.0 154.1 jit_solution(93344198561825827)
XLA Ops:
  0.0 153.2 %moe.1 = (bf16[256,2048]{1,0:T(8,128)(2,1)S(1)}, bf16[2,256,2048]{2,1,0:T(8,128)(2,1)}, bf16[2,256,2048]{2,1,0:T(8,128)(2,1)}) custom-call(s32[2,256]{1,0:T(2,128)} %bitcast.9, f32[2]{0:T(128)} %scale.1, bf16[256,2048]{1,0:T(8,128)(2,1)} %hidh.1, f32[32,2048]{1,0:T(8,128)} %bitcast.8, bf16[2048,2048]{1,0:T(8,128)(2,1)} %bitcast.5, ...), custom_call_target="tpu_custom_call" | custom-call | tf_op jit(solution)/shard_map/moe/pallas_call | solution.py:342
  153.2 1.0 copy.9
